TPU v7x, 32 devices: a whole 2x2x4 slice. The times are simulated.
32 devices in a mesh: shard: 32 (over z, y, x, core).
Axes of the slice: x: 2, y: 2, z: 4, core: 2. Of those that a mesh axis runs over, the one named last changes fastest.
Arguments:
- data_t: bfloat16 [8192, 8192], P('shard'), may hold values from -0.125 to 0.125
- labels: int32 [8192], replicated, may hold values from -1 to 1, as said below
- sample_weight: float32 [8192], replicated, may hold values from 0.1 to 4
- w_start: float32 [8192], P('shard'), may hold values from -10 to 10
- alpha_start: float32 [8192], P('shard'), may hold values from 0 to 1
- visit_order: int32 [64, 128], P('shard'), may hold values from 0 to 127, each once within a row
Outputs:
- weights_out: float32 [8192], P('shard')
- alpha_final: float32 [8192], P('shard')
- objective: float32 [], replicated
Inputs may be any that keep to these rules, and one draw needn't show every extreme that they name: `labels`: each label is -1 or +1. `visit_order`: each row is a permutation of 0 to 127.
All inputs are finite; a program needn't handle non-finite values.
Results may differ from a plain program's by a relative error of at most 0.0047.
Values may be sent and summed in bfloat16 or wider, within the bound.
A program may use at most 64 MiB of HBM per device.

v0:
```python
import functools

import jax
import jax.numpy as jnp
from jax import lax
from jax.experimental import pallas as pl
from jax.experimental.pallas import tpu as pltpu
from jax.sharding import PartitionSpec as P

GROUP = 16
ROWS = 16
MESH = pl.DeviceIdType.MESH
F32 = jnp.float32
BF16 = jnp.bfloat16
HIGH = lax.Precision.HIGHEST


def nn(a, b, precision=None):
    return lax.dot_general(a, b, (((1,), (0,)), ((), ())), preferred_element_type=F32, precision=precision)


def nt(a, b, precision=None):
    return lax.dot_general(a, b, (((1,), (1,)), ((), ())), preferred_element_type=F32, precision=precision)


def spread(row):
    return jnp.broadcast_to(row, (ROWS, row.shape[-1])).astype(BF16)


def kernel(
    devices, data_hbm, label_ref, bound_ref, start_ref, frac_ref, visit_ref,
    out_ref,
    part0, part1, part2, got0, got1, got2, own0, own1, own2, all0, all1, all2,
    data_ref, gram, in_a, in_b, in_c, sum_a, sum_b, sum_c, gram_in,
    load_sem, send_sem, recv_sem, gather_sem, send_a, recv_a, send_b, recv_b, send_c, recv_c, gram_send, gram_recv,
):
    me = lax.axis_index("shard")
    feats, samples = data_hbm.shape
    rows = label_ref.shape[2]
    blocks, block = visit_ref.shape
    features = feats * devices
    cubes = devices // 8
    cube = me // 8
    bit0, bit1, bit2 = me % 2, (me // 2) % 2, (me // 4) % 2
    partner = me + 1 - 2 * bit0

    def columns(k):
        return pl.ds(pl.multiple_of(k * rows, rows), rows)

    def loop(first, last, action):
        def step(i, carry):
            action(i)
            return carry

        lax.fori_loop(first, last, step, 0)

    upward = cube // (cubes // 2)

    def near(i):
        place = upward * (cubes - 2 - i) + (1 - upward) * i
        return place + jnp.where(place >= cube, 1, 0)

    def far(i):
        return near(cubes - 2 - i)

    def mates(action):
        loop(1, 8, lambda i: action(8 * cube + lax.rem(me + i, 8)))

    def cube_of(q, action):
        loop(0, 8, lambda j: action(8 * q + j))

    def peers(action):
        loop(0, cubes - 1, lambda i: cube_of(far(i), action))
        mates(action)

    def remote(source, target, send, recv, peer):
        return pltpu.make_async_remote_copy(
            src_ref=source, dst_ref=target, send_sem=send, recv_sem=recv,
            device_id=(peer,), device_id_type=MESH,
        )

    def total_wait(ref, phase):
        view = ref.at[pl.ds(0, devices - 1)]
        return remote(view, view, send_sem.at[phase], recv_sem.at[phase % 3], partner)

    def scatter_send(part, got, phase):
        def send(peer):
            remote(part.at[peer], got.at[me], send_sem.at[phase], recv_sem.at[phase], peer).start()

        return send

    def gather_start(own, everyone, phase):
        everyone[me] = own[...]
        spot = (phase - 3) * cubes + cube
        peers(lambda peer: remote(own, everyone.at[me], send_sem.at[phase], gather_sem.at[spot], peer).start())

    def part_of(lhs, part, q):
        for j in range(8):
            k = 8 * q + j
            part[k, 0:1, :] = nn(lhs, data_ref[:, columns(k)])[0:1, :]

    def margin_scatter(row, part, got, phase):
        lhs = spread(row)
        send = scatter_send(part, got, phase)

        def step(i):
            q = far(i)
            part_of(lhs, part, q)
            cube_of(q, send)

        loop(0, cubes - 1, step)
        part_of(lhs, part, cube)
        mates(send)
        got[me] = part[me]

    def back(everyone, phase):
        def arrival(q, count):
            view = everyone.at[pl.ds(8 * q, count)]
            spot = (phase - 3) * cubes + q
            remote(view, view, send_sem.at[phase], gather_sem.at[spot], partner).wait_recv()

        def cube_sum(q, total):
            for j in range(8):
                k = 8 * q + j
                total = total + nt(spread(everyone[k][0:1, 0:rows]), data_ref[:, columns(k)])
            return total

        def step(i, total):
            q = near(i)
            arrival(q, 8)
            return cube_sum(q, total)

        arrival(cube, 7)
        total = cube_sum(cube, jnp.zeros((ROWS, feats), F32))
        return lax.fori_loop(0, cubes - 1, step, total)[0:1, :]

    def load(q):
        view = pl.ds(pl.multiple_of(8 * q * rows, rows), 8 * rows)
        return pltpu.make_async_copy(data_hbm.at[:, view], data_ref.at[:, view], load_sem.at[q])

    loop(0, cubes - 1, lambda i: load(far(i)).start())
    load(cube).start()
    barrier = pltpu.get_barrier_semaphore()
    peers(lambda peer: pl.semaphore_signal(barrier, inc=1, device_id=(peer,), device_id_type=MESH))

    w_start = start_ref[...]
    sign, bound = label_ref[me].astype(F32), bound_ref[me]
    start_rows = spread(w_start)

    def first_part(q):
        load(q).wait()
        part_of(start_rows, part0, q)

    loop(0, cubes - 1, lambda i: first_part(far(i)))
    first_part(cube)
    pl.semaphore_wait(barrier, devices - 1)
    peers(scatter_send(part0, got0, 0))
    got0[me] = part0[me]

    row_at = lax.broadcasted_iota(jnp.int32, (block, block), 0)
    lane_at = lax.broadcasted_iota(jnp.int32, (block, block), 1)
    upper, lower, even = row_at < lane_at, row_at > lane_at, row_at == lane_at

    def gram_of(k):
        tile = data_ref[:, columns(k)]
        first, second = tile[:, :block], tile[:, block:]
        top = lax.dot_general(first, tile, (((0,), (0,)), ((), ())), preferred_element_type=F32)
        low = lax.dot_general(second, second, (((0,), (0,)), ((), ())), preferred_element_type=F32)
        gram[k, :, :block] = jnp.where(upper, top[:, :block], low).astype(BF16)
        gram[k, :, block:] = top[:, block:].astype(BF16)
        part1[k, 1:2, :block] = jnp.sum(jnp.where(even, top[:, :block], 0.0), axis=0, keepdims=True)
        part1[k, 1:2, block:] = jnp.sum(jnp.where(even, low, 0.0), axis=0, keepdims=True)
        left, right = first.astype(F32), second.astype(F32)
        return left * left + right * right

    def halving(source, target, index, sends, recvs, peer):
        return pltpu.make_async_remote_copy(
            src_ref=source, dst_ref=target.at[index], send_sem=sends.at[index],
            recv_sem=recvs.at[index], device_id=(peer,), device_id_type=MESH,
        )

    def copy_a(q, j):
        return halving(gram.at[8 * q + 2 * j + 1 - bit0], in_a, 4 * q + j, send_a, recv_a, partner)

    def order_of(q):
        swap = q % 2
        return (1 - swap) * bit1 + swap * bit2, 1 + swap, (1 - swap) * bit2 + swap * bit1, 2 - swap

    def copy_b(q, t):
        bit, weight, _, other = order_of(q)
        return halving(
            sum_a.at[4 * q + weight * (1 - bit) + other * t], in_b, 2 * q + t, send_b, recv_b,
            me + 2 * weight * (1 - 2 * bit),
        )

    def copy_c(q):
        _, _, bit, weight = order_of(q)
        return halving(sum_b.at[2 * q + 1 - bit], in_c, q, send_c, recv_c, me + 2 * weight * (1 - 2 * bit))

    def copy_d(q):
        return pltpu.make_async_remote_copy(
            src_ref=sum_c.at[q], dst_ref=gram_in.at[cube], send_sem=gram_send.at[0],
            recv_sem=gram_recv.at[0], device_id=(me + 8 * (q - cube),), device_id_type=MESH,
        )

    def added(x, y):
        return (x.astype(F32) + y.astype(F32)).astype(BF16)

    def turn(i):
        return jnp.where(i == cubes - 1, cube, far(jnp.minimum(i, cubes - 2)))

    def merge_a(i):
        q = turn(i)
        bit, weight, last, other = order_of(q)
        for t in (1 - last, last):
            for side in (1 - bit, bit):
                at = weight * side + other * t
                copy_a(q, at).wait_recv()
                sum_a[4 * q + at] = added(gram[8 * q + 2 * at + bit0], in_a[4 * q + at])
            copy_b(q, t).start()

    def merge_b(i):
        q = turn(i)
        bit, weight, last, other = order_of(q)
        for t in (1 - last, last):
            copy_b(q, t).wait_recv()
            sum_b[2 * q + t] = added(sum_a[4 * q + weight * bit + other * t], in_b[2 * q + t])
        copy_c(q).start()

    def merged_c(q):
        bit = order_of(q)[2]
        copy_c(q).wait_recv()
        return added(sum_b[2 * q + bit], in_c[q])

    def merge_c(i):
        q = turn(i)
        sum_c[q] = merged_c(q)
        copy_d(q).start()

    def gram_step(i, total):
        q = turn(i)
        for j in range(4):
            total = total + gram_of(8 * q + 2 * j + 1 - bit0)
        for j in range(4):
            copy_a(q, j).start()
        for j in range(4):
            total = total + gram_of(8 * q + 2 * j + bit0)
        merge_a(i)
        return total

    half = cubes // 2
    square_total = lax.fori_loop(0, half, gram_step, jnp.zeros((feats, block), F32))
    total_wait(got0, 0).wait_recv()
    margin0 = jnp.sum(got0[...], axis=0)
    own0[...] = bound * sign * jnp.maximum(0.0, 1.0 - sign * margin0)
    gather_start(own0, all0, 0 + 3)

    def late_step(i, total):
        total = gram_step(i, total)
        merge_b(i - half)
        return total

    square_total = lax.fori_loop(half, cubes, late_step, square_total)
    column_sq = nt(jnp.ones((8, block), F32), square_total, HIGH)[0:1, :]
    ascent = back(all0, 3)
    loop(cubes - half, cubes - 1, merge_b)
    scale = column_sq / samples + 1e-06
    stepped = w_start + ascent / (samples * scale)
    thresh = 1.0 / (4.0 * features * scale)
    primal = stepped - jnp.clip(stepped, -thresh, thresh)
    margin_scatter(primal, part1, got1, 1)
    merge_b(cubes - 1)
    loop(0, cubes - 1, merge_c)
    gram_in[cube] = merged_c(cube)

    orders, places = [], []
    for b in range(blocks):
        order = (lax.broadcasted_iota(jnp.int32, (block, block), 0) == visit_ref[b:b + 1, :]).astype(F32)
        orders.append(order)
        places.append(order.T.astype(BF16))

    alpha_zero = bound * frac_ref[...]

    def permute(vectors):
        stacked = jnp.concatenate(list(vectors) + [jnp.zeros((8 - len(vectors), rows), F32)], axis=0)
        return [nn(stacked[:, b * block:(b + 1) * block], orders[b], HIGH) for b in range(blocks)]

    total_wait(got1, 1).wait_recv()
    received = jnp.sum(got1[...], axis=0)
    margin1, diag = received[0:1, :], received[1:2, :]
    loss = jnp.sum(bound * jnp.square(jnp.maximum(0.0, 1.0 - sign * margin1)), axis=1, keepdims=True)
    penalty = jnp.sum(jnp.abs(primal), axis=1, keepdims=True)
    objective_part = loss / (2.0 * samples) + penalty / (4.0 * features)
    permuted = permute((sign, bound, alpha_zero, diag, margin1))
    sign_p = [x[0:1] for x in permuted]
    bound_p = [x[1:2] for x in permuted]
    zero_p = [x[2:3] for x in permuted]
    inverse_p = [0.5 / (x[3:4] + 1e-06) for x in permuted]
    margin_p = [x[4:5] for x in permuted]

    view = gram_in.at[pl.ds(0, cubes - 1)]
    gram_wait = pltpu.make_async_remote_copy(
        src_ref=view, dst_ref=view, send_sem=gram_send.at[0], recv_sem=gram_recv.at[0],
        device_id=(partner,), device_id_type=MESH,
    )
    gram_wait.wait_recv()
    full = jnp.sum(gram_in[...].astype(F32), axis=0)
    packed, cross = full[:, :block], full[:, block:]
    above, below = jnp.where(upper, packed, 0.0), jnp.where(lower, packed, 0.0)
    blocks_p = {}
    for (a, b), piece in {(0, 0): above + above.T, (0, 1): cross, (1, 1): below + below.T}.items():
        piece = nn(piece.astype(BF16), orders[b].astype(BF16)).astype(BF16)
        blocks_p[a, b] = nn(places[a], piece).astype(BF16)

    lane = lax.broadcasted_iota(jnp.int32, (1, block), 1)
    sub = lax.broadcasted_iota(jnp.int32, (ROWS, block), 0)

    def times_gram(delta, piece):
        high = delta.astype(BF16).astype(F32)
        lhs = jnp.where(sub == 0, high, jnp.where(sub == 1, delta - high, 0.0)).astype(BF16)
        return 2.0 * jnp.sum(nn(lhs, piece)[0:8], axis=0, keepdims=True)

    def sweep(alpha, margin):
        result, margin = [], list(margin)
        for b in range(blocks):
            now, m, moved = alpha[b], margin[b], jnp.zeros((1, block), F32)
            for s in range(block // GROUP):
                fresh = jnp.clip(now + (1.0 - sign_p[b] * m) * inverse_p[b], 0.0, bound_p[b])
                mine = (lane >= s * GROUP) & (lane < (s + 1) * GROUP)
                change = jnp.where(mine, fresh - now, 0.0)
                now = jnp.where(mine, fresh, now)
                change = sign_p[b] * change
                moved = moved + change
                if s + 1 < block // GROUP:
                    m = m + times_gram(change, blocks_p[b, b])
            for later in range(b + 1, blocks):
                margin[later] = margin[later] + times_gram(moved, blocks_p[b, later])
            result.append(now)
        return result

    def changes(after, before):
        pieces = []
        for b in range(blocks):
            z = spread(sign_p[b] * (after[b] - before[b]))
            pieces.append(nt(z, orders[b].astype(BF16))[0:1, :])
        return jnp.concatenate(pieces, axis=1)

    one_p = sweep(zero_p, margin_p)
    own1[0:1, 0:rows] = changes(one_p, zero_p)
    own1[0:1, rows:] = jnp.broadcast_to(objective_part, (1, block))
    gather_start(own1, all1, 1 + 3)
    update_one = back(all1, 4) * (2.0 / devices)
    margin_scatter(update_one, part2, got2, 2)
    out_ref[:, feats + rows:] = jnp.sum(all1[...], axis=0)[:, rows:]
    total_wait(got2, 2).wait_recv()
    margin2 = margin1 + jnp.sum(got2[...], axis=0)
    margin2_p = [x[0:1] for x in permute((margin2,))]
    two_p = sweep(one_p, margin2_p)
    own2[...] = changes(two_p, one_p)
    gather_start(own2, all2, 2 + 3)
    for b in range(blocks):
        spot = jnp.broadcast_to(two_p[b], (8, block))
        out_ref[:, feats + b * block:feats + (b + 1) * block] = nt(spot, orders[b], HIGH)[0:1, :]
    out_ref[:, :feats] = primal + update_one + back(all2, 5) * (2.0 / devices)

    for phase, ref in enumerate((got0, got1, got2)):
        total_wait(ref, phase).wait_send()
    for phase, ref in enumerate((all0, all1, all2)):
        total_wait(ref, phase + 3).wait_send()
    gram_wait.wait_send()

    def drain(q):
        for j in range(4):
            copy_a(q, j).wait_send()
        for j in range(2):
            copy_b(q, j).wait_send()
        copy_c(q).wait_send()

    loop(0, cubes, drain)


def body(devices, data_t, labels, sample_weight, w_start, alpha_start, visit_order):
    feats = data_t.shape[0]
    rows = alpha_start.shape[0]
    blocks, block = visit_order.shape
    cubes = devices // 8
    labels = labels.reshape(devices, 1, rows)
    bound = sample_weight.reshape(devices, 1, rows)

    def grams(count):
        return pltpu.VMEM((count, block, rows), BF16)

    def semaphores(count):
        return pltpu.SemaphoreType.DMA((count,))

    def vectors(height, length):
        return pltpu.VMEM((devices, height, length), F32)

    vmem = pl.BlockSpec(memory_space=pltpu.VMEM)
    out = pl.pallas_call(
        functools.partial(kernel, devices),
        name="svm_rounds",
        out_shape=jax.ShapeDtypeStruct((1, feats + rows + block), F32),
        in_specs=[pl.BlockSpec(memory_space=pl.ANY)] + [vmem] * 5,
        out_specs=vmem,
        scratch_shapes=[
            vectors(1, rows), vectors(2, rows), vectors(1, rows),
            vectors(1, rows), vectors(2, rows), vectors(1, rows),
            pltpu.VMEM((1, rows), F32), pltpu.VMEM((1, rows + block), F32), pltpu.VMEM((1, rows), F32),
            vectors(1, rows), vectors(1, rows + block), vectors(1, rows),
            pltpu.VMEM(data_t.shape, BF16), grams(devices), grams(4 * cubes), grams(2 * cubes), grams(cubes),
            grams(4 * cubes), grams(2 * cubes), grams(cubes), grams(cubes),
            semaphores(cubes), semaphores(6), semaphores(3), semaphores(3 * cubes), semaphores(4 * cubes), semaphores(4 * cubes),
            semaphores(2 * cubes), semaphores(2 * cubes), semaphores(cubes), semaphores(cubes),
            semaphores(1), semaphores(1),
        ],
        compiler_params=pltpu.CompilerParams(
            collective_id=0, has_side_effects=True, vmem_limit_bytes=63 * 1024 * 1024
        ),
    )(data_t, labels, bound, w_start[None], alpha_start[None], visit_order)
    return out[0, :feats], out[0, feats:feats + rows], out[0, feats + rows]


def solution(mesh):
    placed = (P("shard", None), P(), P(), P("shard"), P("shard"), P("shard", None))
    return jax.shard_map(
        functools.partial(body, mesh.shape["shard"]), mesh=mesh, in_specs=placed,
        out_specs=(P("shard"), P("shard"), P()), check_vma=False,
    )
```

profile of v0, /device:TPU:0, one launch (start us, length us, event | category | flops | bytes accessed | tf_op | source)
XLA Modules:
  0.0 51.9 jit_solution(15864742732937940862)
XLA Ops:
  0.6 48.9 %svm_rounds.1 = f32[1,640]{1,0:T(1,128)} custom-call(bf16[256,8192]{1,0:T(8,128)(2,1)} %data_hbm.1, s32[32,1,256]{2,1,0:T(1,128)} %bitcast.7, f32[32,1,256]{2,1,0:T(1,128)} %bitcast.8, f32[1,256]{1,0:T(1,128)} %bitcast.9, f32[1,256]{1,0:T(1,128)} %bitcast.10, s32[2,128]{1,0:T(2,128)} %visit_ref.1), custom_call_target="tpu_custom_call" | custom-call | tf_op jit(solution)/shard_map/svm_rounds/pallas_call | solution.py:400
  49.5 1.2 %fusion = (f32[1,256]{1,0:T(1,128)}, f32[1,256]{1,0:T(1,128)}) fusion(f32[1,640]{1,0:T(1,128)} %svm_rounds.1), kind=kLoop, calls=%fused_computation | loop fusion | bytes 4096 | tf_op jit(solution)/shard_map/slice | solution.py:421
  50.8 1.2 %slice.11 = f32[1,1]{1,0:T(1,128)} slice(f32[1,640]{1,0:T(1,128)} %svm_rounds.1), slice={[0:1], [512:513]} | slice | bytes 8 | tf_op jit(solution)/shard_map/slice | solution.py:421
where the time goes:
time: 52.2 us; the launch traced here: 51.9 us
  Pallas kernels  48.9 us (94%)
  local copies, waits for them, and re-layouts  2.41 us (5%)
  between operations  0.64 us (1%)
    pallas_call x1, Pallas kernels, body(): pl.pallas_call(functools.partial(kernel, devices), name='svm_rounds', out...  48.9 us
    slice x2, local copies, waits for them, and re-layouts, body(): return (out[0, :feats], out[0, feats:feats + rows], out[0, feats + rows])  2.41 us

commit v1 on v0

--- a/solution.py
+++ b/solution.py
@@ -28,16 +28,16 @@
 
 
 def kernel(
-    devices, data_hbm, label_ref, bound_ref, start_ref, frac_ref, visit_ref,
+    devices, data_hbm, label_hbm, bound_hbm, start_hbm, frac_hbm, visit_hbm,
     out_ref,
     part0, part1, part2, got0, got1, got2, own0, own1, own2, all0, all1, all2,
-    data_ref, gram, in_a, in_b, in_c, sum_a, sum_b, sum_c, gram_in,
-    load_sem, send_sem, recv_sem, gather_sem, send_a, recv_a, send_b, recv_b, send_c, recv_c, gram_send, gram_recv,
+    data_ref, label_ref, bound_ref, start_ref, frac_ref, visit_ref, squares, gram, in_a, in_b, in_c, sum_a, sum_b, sum_c, gram_in,
+    load_sem, small_sem, send_sem, recv_sem, gather_sem, send_a, recv_a, send_b, recv_b, send_c, recv_c, gram_send, gram_recv,
 ):
     me = lax.axis_index("shard")
     feats, samples = data_hbm.shape
-    rows = label_ref.shape[2]
-    blocks, block = visit_ref.shape
+    rows = label_hbm.shape[2]
+    blocks, block = visit_hbm.shape
     features = feats * devices
     cubes = devices // 8
     cube = me // 8
@@ -113,7 +113,7 @@
         mates(send)
         got[me] = part[me]
 
-    def back(everyone, phase):
+    def back(everyone, phase, meanwhile=None):
         def arrival(q, count):
             view = everyone.at[pl.ds(8 * q, count)]
             spot = (phase - 3) * cubes + q
@@ -132,30 +132,28 @@
 
         arrival(cube, 7)
         total = cube_sum(cube, jnp.zeros((ROWS, feats), F32))
+        if meanwhile is not None:
+            meanwhile()
         return lax.fori_loop(0, cubes - 1, step, total)[0:1, :]
 
     def load(q):
         view = pl.ds(pl.multiple_of(8 * q * rows, rows), 8 * rows)
         return pltpu.make_async_copy(data_hbm.at[:, view], data_ref.at[:, view], load_sem.at[q])
 
+    small = [
+        pltpu.make_async_copy(source, target, small_sem.at[i])
+        for i, (source, target) in enumerate((
+            (start_hbm, start_ref), (label_hbm.at[me], label_ref), (bound_hbm.at[me], bound_ref),
+            (frac_hbm, frac_ref), (visit_hbm, visit_ref),
+        ))
+    ]
+    small[0].start()
     loop(0, cubes - 1, lambda i: load(far(i)).start())
     load(cube).start()
+    for copy in small[1:]:
+        copy.start()
     barrier = pltpu.get_barrier_semaphore()
     peers(lambda peer: pl.semaphore_signal(barrier, inc=1, device_id=(peer,), device_id_type=MESH))
-
-    w_start = start_ref[...]
-    sign, bound = label_ref[me].astype(F32), bound_ref[me]
-    start_rows = spread(w_start)
-
-    def first_part(q):
-        load(q).wait()
-        part_of(start_rows, part0, q)
-
-    loop(0, cubes - 1, lambda i: first_part(far(i)))
-    first_part(cube)
-    pl.semaphore_wait(barrier, devices - 1)
-    peers(scatter_send(part0, got0, 0))
-    got0[me] = part0[me]
 
     row_at = lax.broadcasted_iota(jnp.int32, (block, block), 0)
     lane_at = lax.broadcasted_iota(jnp.int32, (block, block), 1)
@@ -170,8 +168,6 @@
         gram[k, :, block:] = top[:, block:].astype(BF16)
         part1[k, 1:2, :block] = jnp.sum(jnp.where(even, top[:, :block], 0.0), axis=0, keepdims=True)
         part1[k, 1:2, block:] = jnp.sum(jnp.where(even, low, 0.0), axis=0, keepdims=True)
-        left, right = first.astype(F32), second.astype(F32)
-        return left * left + right * right
 
     def halving(source, target, index, sends, recvs, peer):
         return pltpu.make_async_remote_copy(
@@ -182,19 +178,21 @@
     def copy_a(q, j):
         return halving(gram.at[8 * q + 2 * j + 1 - bit0], in_a, 4 * q + j, send_a, recv_a, partner)
 
-    def order_of(q):
-        swap = q % 2
+    def order_of(i):
+        swap = i % 2
         return (1 - swap) * bit1 + swap * bit2, 1 + swap, (1 - swap) * bit2 + swap * bit1, 2 - swap
 
-    def copy_b(q, t):
-        bit, weight, _, other = order_of(q)
+    def copy_b(i, t):
+        q = turn(i)
+        bit, weight, _, other = order_of(i)
         return halving(
             sum_a.at[4 * q + weight * (1 - bit) + other * t], in_b, 2 * q + t, send_b, recv_b,
             me + 2 * weight * (1 - 2 * bit),
         )
 
-    def copy_c(q):
-        _, _, bit, weight = order_of(q)
+    def copy_c(i):
+        q = turn(i)
+        _, _, bit, weight = order_of(i)
         return halving(sum_b.at[2 * q + 1 - bit], in_c, q, send_c, recv_c, me + 2 * weight * (1 - 2 * bit))
 
     def copy_d(q):
@@ -211,67 +209,104 @@
 
     def merge_a(i):
         q = turn(i)
-        bit, weight, last, other = order_of(q)
+        bit, weight, last, other = order_of(i)
         for t in (1 - last, last):
             for side in (1 - bit, bit):
                 at = weight * side + other * t
                 copy_a(q, at).wait_recv()
                 sum_a[4 * q + at] = added(gram[8 * q + 2 * at + bit0], in_a[4 * q + at])
-            copy_b(q, t).start()
+            copy_b(i, t).start()
 
     def merge_b(i):
         q = turn(i)
-        bit, weight, last, other = order_of(q)
+        bit, weight, last, other = order_of(i)
         for t in (1 - last, last):
-            copy_b(q, t).wait_recv()
+            copy_b(i, t).wait_recv()
             sum_b[2 * q + t] = added(sum_a[4 * q + weight * bit + other * t], in_b[2 * q + t])
-        copy_c(q).start()
-
-    def merged_c(q):
-        bit = order_of(q)[2]
-        copy_c(q).wait_recv()
+        copy_c(i).start()
+
+    def merged_c(i):
+        q = turn(i)
+        bit = order_of(i)[2]
+        copy_c(i).wait_recv()
         return added(sum_b[2 * q + bit], in_c[q])
 
     def merge_c(i):
         q = turn(i)
-        sum_c[q] = merged_c(q)
+        sum_c[q] = merged_c(i)
         copy_d(q).start()
 
-    def gram_step(i, total):
-        q = turn(i)
+    def start_a(i):
         for j in range(4):
-            total = total + gram_of(8 * q + 2 * j + 1 - bit0)
+            copy_a(turn(i), j).start()
+
+    def gram_part(i, side):
         for j in range(4):
-            copy_a(q, j).start()
-        for j in range(4):
-            total = total + gram_of(8 * q + 2 * j + bit0)
-        merge_a(i)
-        return total
-
-    half = cubes // 2
-    square_total = lax.fori_loop(0, half, gram_step, jnp.zeros((feats, block), F32))
+            gram_of(8 * turn(i) + 2 * j + side)
+
+    def gram_step(i):
+        gram_part(i, 1 - bit0)
+        start_a(i)
+        gram_part(i, bit0)
+
+    small[0].wait()
+    w_start = start_ref[...]
+    start_rows = spread(w_start)
+
+    def add_squares(q):
+        for r in range(0, feats, 32):
+            total = squares[r:r + 32, :]
+            for j in range(8 * blocks):
+                at = pl.ds(pl.multiple_of(8 * q * rows + j * block, block), block)
+                piece = data_ref[r:r + 32, at].astype(F32)
+                total = total + piece * piece
+            squares[r:r + 32, :] = total
+
+    def first_part(q):
+        load(q).wait()
+        part_of(start_rows, part0, q)
+
+    first_part(far(0))
+    gram_part(0, 1 - bit0)
+    gram_part(0, bit0)
+    loop(1, cubes - 1, lambda i: first_part(far(i)))
+    first_part(cube)
+    pl.semaphore_wait(barrier, devices - 1)
+    peers(scatter_send(part0, got0, 0))
+    got0[me] = part0[me]
+    start_a(0)
+
+    def early_step(i):
+        gram_step(i)
+        merge_a(i - 1)
+
+    loop(1, cubes - 1, early_step)
+    gram_step(cubes - 1)
+    squares[...] = jnp.zeros((feats, block), F32)
+    loop(0, cubes, add_squares)
+    for copy in small[1:]:
+        copy.wait()
+    sign, bound = label_ref[...].astype(F32), bound_ref[...]
     total_wait(got0, 0).wait_recv()
     margin0 = jnp.sum(got0[...], axis=0)
     own0[...] = bound * sign * jnp.maximum(0.0, 1.0 - sign * margin0)
     gather_start(own0, all0, 0 + 3)
-
-    def late_step(i, total):
-        total = gram_step(i, total)
-        merge_b(i - half)
-        return total
-
-    square_total = lax.fori_loop(half, cubes, late_step, square_total)
+    merge_a(cubes - 2)
+    loop(0, cubes - 2, merge_b)
+    merge_a(cubes - 1)
+    square_total = squares[...]
     column_sq = nt(jnp.ones((8, block), F32), square_total, HIGH)[0:1, :]
     ascent = back(all0, 3)
-    loop(cubes - half, cubes - 1, merge_b)
     scale = column_sq / samples + 1e-06
     stepped = w_start + ascent / (samples * scale)
     thresh = 1.0 / (4.0 * features * scale)
     primal = stepped - jnp.clip(stepped, -thresh, thresh)
     margin_scatter(primal, part1, got1, 1)
+    merge_b(cubes - 2)
+    merge_c(0)
     merge_b(cubes - 1)
-    loop(0, cubes - 1, merge_c)
-    gram_in[cube] = merged_c(cube)
+    loop(1, cubes - 1, merge_c)
+    gram_in[cube] = merged_c(cubes - 1)
 
     orders, places = [], []
     for b in range(blocks):
@@ -358,10 +393,12 @@
     two_p = sweep(one_p, margin2_p)
     own2[...] = changes(two_p, one_p)
     gather_start(own2, all2, 2 + 3)
-    for b in range(blocks):
-        spot = jnp.broadcast_to(two_p[b], (8, block))
-        out_ref[:, feats + b * block:feats + (b + 1) * block] = nt(spot, orders[b], HIGH)[0:1, :]
-    out_ref[:, :feats] = primal + update_one + back(all2, 5) * (2.0 / devices)
+    def alpha_out():
+        for b in range(blocks):
+            spot = jnp.broadcast_to(two_p[b], (8, block))
+            out_ref[:, feats + b * block:feats + (b + 1) * block] = nt(spot, orders[b], HIGH)[0:1, :]
+
+    out_ref[:, :feats] = primal + update_one + back(all2, 5, alpha_out) * (2.0 / devices)
 
     for phase, ref in enumerate((got0, got1, got2)):
         total_wait(ref, phase).wait_send()
@@ -369,14 +406,21 @@
         total_wait(ref, phase + 3).wait_send()
     gram_wait.wait_send()
 
-    def drain(q):
+    def drain(i):
         for j in range(4):
-            copy_a(q, j).wait_send()
+            copy_a(turn(i), j).wait_send()
         for j in range(2):
-            copy_b(q, j).wait_send()
-        copy_c(q).wait_send()
+            copy_b(i, j).wait_send()
+        copy_c(i).wait_send()
 
     loop(0, cubes, drain)
+
+
+def split(packed, weights, alpha, objective):
+    feats, rows = weights.shape[1], alpha.shape[1]
+    weights[...] = packed[:, :feats]
+    alpha[...] = packed[:, feats:feats + rows]
+    objective[...] = packed[:, feats + rows:feats + rows + 1]
 
 
 def body(devices, data_t, labels, sample_weight, w_start, alpha_start, visit_order):
@@ -401,16 +445,18 @@
         functools.partial(kernel, devices),
         name="svm_rounds",
         out_shape=jax.ShapeDtypeStruct((1, feats + rows + block), F32),
-        in_specs=[pl.BlockSpec(memory_space=pl.ANY)] + [vmem] * 5,
+        in_specs=[pl.BlockSpec(memory_space=pl.ANY)] * 6,
         out_specs=vmem,
         scratch_shapes=[
             vectors(1, rows), vectors(2, rows), vectors(1, rows),
             vectors(1, rows), vectors(2, rows), vectors(1, rows),
             pltpu.VMEM((1, rows), F32), pltpu.VMEM((1, rows + block), F32), pltpu.VMEM((1, rows), F32),
             vectors(1, rows), vectors(1, rows + block), vectors(1, rows),
-            pltpu.VMEM(data_t.shape, BF16), grams(devices), grams(4 * cubes), grams(2 * cubes), grams(cubes),
+            pltpu.VMEM(data_t.shape, BF16), pltpu.VMEM((1, rows), jnp.int32), pltpu.VMEM((1, rows), F32),
+            pltpu.VMEM((1, feats), F32), pltpu.VMEM((1, rows), F32), pltpu.VMEM((blocks, block), jnp.int32),
+            pltpu.VMEM((feats, block), F32), grams(devices), grams(4 * cubes), grams(2 * cubes), grams(cubes),
             grams(4 * cubes), grams(2 * cubes), grams(cubes), grams(cubes),
-            semaphores(cubes), semaphores(6), semaphores(3), semaphores(3 * cubes), semaphores(4 * cubes), semaphores(4 * cubes),
+            semaphores(cubes), semaphores(5), semaphores(6), semaphores(3), semaphores(3 * cubes), semaphores(4 * cubes), semaphores(4 * cubes),
             semaphores(2 * cubes), semaphores(2 * cubes), semaphores(cubes), semaphores(cubes),
             semaphores(1), semaphores(1),
         ],
@@ -418,7 +464,16 @@
             collective_id=0, has_side_effects=True, vmem_limit_bytes=63 * 1024 * 1024
         ),
     )(data_t, labels, bound, w_start[None], alpha_start[None], visit_order)
-    return out[0, :feats], out[0, feats:feats + rows], out[0, feats + rows]
+    weights, alpha, objective = pl.pallas_call(
+        split,
+        name="split",
+        out_shape=(
+            jax.ShapeDtypeStruct((1, feats), F32), jax.ShapeDtypeStruct((1, rows), F32), jax.ShapeDtypeStruct((1, 1), F32)
+        ),
+        in_specs=[vmem],
+        out_specs=(vmem, vmem, vmem),
+    )(out)
+    return weights[0], alpha[0], objective[0, 0]
 
 
 def solution(mesh):

time: 52.2 us -> 48.7 us (0.933)
  local copies, waits for them, and re-layouts: 2.41 us -> 0 us
  Pallas kernels: 48.9 us -> 47.9 us
    slice x2 -> x0, local copies, waits for them, and re-layouts: 2.41 us -> none  [body(): return (out[0, :feats], out[0, feats:feats + rows], out[0, feats + rows])]
    pallas_call x1, Pallas kernels: 48.9 us -> 46.7 us  [body(): pl.pallas_call(functools.partial(kernel, devices), name='svm_rounds', out...]
    pallas_call x0 -> x1, Pallas kernels: none -> 1.24 us  [body(): pl.pallas_call(split, name='split', out_shape=(jax.ShapeDtypeStruct((1, f...]
where the time goes in v1:
time: 48.7 us; the launch traced here: 48.6 us
  Pallas kernels  47.9 us (98%)
  between operations  0.64 us (1%)
    pallas_call x1, Pallas kernels, body(): pl.pallas_call(functools.partial(kernel, devices), name='svm_rounds', out...  46.7 us
    pallas_call x1, Pallas kernels, body(): pl.pallas_call(split, name='split', out_shape=(jax.ShapeDtypeStruct((1, f...  1.24 us

profile of v1, /device:TPU:0, one launch (start us, length us, event | category | flops | bytes accessed | tf_op | source)
XLA Modules:
  0.0 48.6 jit_solution(13055119237719071233)
XLA Ops:
  0.6 46.7 %svm_rounds.1.packed = f32[1,640]{1,0:T(1,128)} custom-call(bf16[256,8192]{1,0:T(8,128)(2,1)} %data_hbm.1, s32[32,1,256]{2,1,0:T(1,128)} %bitcast.7, f32[32,1,256]{2,1,0:T(1,128)} %bitcast.8, f32[1,256]{1,0:T(1,128)} %bitcast.9, f32[1,256]{1,0:T(1,128)} %bitcast.10, s32[2,128]{1,0:T(2,128)} %visit_hbm.1), custom_call_target="tpu_custom_call" | custom-call | tf_op jit(solution)/shard_map/svm_rounds/pallas_call | solution.py:444
  47.3 1.2 %split.1 = (f32[1,256]{1,0:T(1,128)}, f32[1,256]{1,0:T(1,128)}, f32[1,1]{1,0:T(1,128)}) custom-call(f32[1,640]{1,0:T(1,128)} %svm_rounds.1.packed), custom_call_target="tpu_custom_call" | custom-call | tf_op jit(solution)/shard_map/split/pallas_call | solution.py:467

commit v2 on v1

--- a/solution.py
+++ b/solution.py
@@ -28,10 +28,11 @@
 
 
 def kernel(
-    devices, data_hbm, label_hbm, bound_hbm, start_hbm, frac_hbm, visit_hbm,
+    devices, data_hbm, label_hbm, bound_hbm, label_tiles, bound_tiles, start_hbm, frac_hbm, visit_hbm,
     out_ref,
     part0, part1, part2, got0, got1, got2, own0, own1, own2, all0, all1, all2,
-    data_ref, label_ref, bound_ref, start_ref, frac_ref, visit_ref, squares, gram, in_a, in_b, in_c, sum_a, sum_b, sum_c, gram_in,
+    data_ref, label_ref, bound_ref, owned_label, owned_bound, start_ref, frac_ref, visit_ref, squares, gram, in_a, in_b, in_c, sum_a, sum_b, sum_c, gram_in,
+    picks, table, square, sign_c, bound_c, inverse_c, alpha_c, margin_c,
     load_sem, small_sem, send_sem, recv_sem, gather_sem, send_a, recv_a, send_b, recv_b, send_c, recv_c, gram_send, gram_recv,
 ):
     me = lax.axis_index("shard")
@@ -55,6 +56,11 @@
         lax.fori_loop(first, last, step, 0)
 
     upward = cube // (cubes // 2)
+    owners = label_tiles.shape[0]
+    held = devices // owners
+    low = cubes // 4
+    is_owner = (cube >= low) & (cube < cubes - low) & (bit0 == 1)
+    mine = jnp.clip(me // 2 - 4 * low, 0, owners - 1)
 
     def near(i):
         place = upward * (cubes - 2 - i) + (1 - upward) * i
@@ -145,6 +151,7 @@
         for i, (source, target) in enumerate((
             (start_hbm, start_ref), (label_hbm.at[me], label_ref), (bound_hbm.at[me], bound_ref),
             (frac_hbm, frac_ref), (visit_hbm, visit_ref),
+            (label_tiles.at[mine], owned_label), (bound_tiles.at[mine], owned_bound),
         ))
     ]
     small[0].start()
@@ -195,10 +202,18 @@
         _, _, bit, weight = order_of(i)
         return halving(sum_b.at[2 * q + 1 - bit], in_c, q, send_c, recv_c, me + 2 * weight * (1 - 2 * bit))
 
-    def copy_d(q):
+    def copy_d(q, half):
+        view = pl.ds(half * block, block)
         return pltpu.make_async_remote_copy(
-            src_ref=sum_c.at[q], dst_ref=gram_in.at[cube], send_sem=gram_send.at[0],
-            recv_sem=gram_recv.at[0], device_id=(me + 8 * (q - cube),), device_id_type=MESH,
+            src_ref=sum_c.at[q, :, view], dst_ref=gram_in.at[cube, :, view], send_sem=gram_send.at[half],
+            recv_sem=gram_recv.at[half], device_id=(me + 8 * (q - cube),), device_id_type=MESH,
+        )
+
+    def wait_d(half):
+        view = gram_in.at[pl.ds(0, cubes - 1), :, pl.ds(half * block, block)]
+        return pltpu.make_async_remote_copy(
+            src_ref=view, dst_ref=view, send_sem=gram_send.at[half], recv_sem=gram_recv.at[half],
+            device_id=(partner,), device_id_type=MESH,
         )
 
     def added(x, y):
@@ -234,7 +249,8 @@
     def merge_c(i):
         q = turn(i)
         sum_c[q] = merged_c(i)
-        copy_d(q).start()
+        copy_d(q, 0).start()
+        copy_d(q, 1).start()
 
     def start_a(i):
         for j in range(4):
@@ -264,7 +280,29 @@
 
     def first_part(q):
         load(q).wait()
-        part_of(start_rows, part0, q)
+        for j in range(8):
+            row = nn(start_rows, data_ref[:, columns(8 * q + j)])
+            for b in range(blocks):
+                at = j % held * blocks + b
+                part0[8 // held * q + j // held, at:at + 1, :] = row[0:1, b * block:(b + 1) * block]
+
+    def each_owner(action):
+        def step(i):
+            o = upward * i + (1 - upward) * (owners - 1 - i)
+            peer = 8 * low + 2 * o + 1
+
+            @pl.when(peer != me)
+            def _():
+                action(o, peer)
+
+        loop(0, owners, step)
+
+    def owned(ref, count):
+        return ref.at[pl.ds(0, count)]
+
+    def waiting(ref, count, send, recv):
+        view = owned(ref, count)
+        return remote(view, view, send, recv, partner)
 
     first_part(far(0))
     gram_part(0, 1 - bit0)
@@ -272,8 +310,7 @@
     loop(1, cubes - 1, lambda i: first_part(far(i)))
     first_part(cube)
     pl.semaphore_wait(barrier, devices - 1)
-    peers(scatter_send(part0, got0, 0))
-    got0[me] = part0[me]
+    each_owner(lambda o, peer: remote(part0.at[o], got0.at[me], send_sem.at[0], recv_sem.at[0], peer).start())
     start_a(0)
 
     def early_step(i):
@@ -287,16 +324,48 @@
     for copy in small[1:]:
         copy.wait()
     sign, bound = label_ref[...].astype(F32), bound_ref[...]
-    total_wait(got0, 0).wait_recv()
-    margin0 = jnp.sum(got0[...], axis=0)
-    own0[...] = bound * sign * jnp.maximum(0.0, 1.0 - sign * margin0)
-    gather_start(own0, all0, 0 + 3)
+
+    @pl.when(is_owner)
+    def _():
+        got0[me] = part0[mine]
+        waiting(got0, devices - 1, send_sem.at[0], recv_sem.at[0]).wait_recv()
+        margin0 = jnp.sum(got0[...], axis=0)
+        side = owned_label[...].astype(F32)
+        own0[...] = (owned_bound[...] * side * jnp.maximum(0.0, 1.0 - side * margin0)).astype(BF16)
+        all0[mine] = own0[...]
+        peers(lambda peer: remote(own0, all0.at[mine], send_sem.at[3], gather_sem.at[cube], peer).start())
+
     merge_a(cubes - 2)
     loop(0, cubes - 2, merge_b)
     merge_a(cubes - 1)
     square_total = squares[...]
     column_sq = nt(jnp.ones((8, block), F32), square_total, HIGH)[0:1, :]
-    ascent = back(all0, 3)
+    def start_sum(i, total):
+        q = low + upward * (cubes - 2 * low - 1 - i) + (1 - upward) * i
+
+        def wait(count):
+            view = all0.at[pl.ds(0, count)]
+            remote(view, view, send_sem.at[3], gather_sem.at[q], partner).wait_recv()
+
+        own_turn = is_owner & (q == cube)
+
+        @pl.when(own_turn)
+        def _():
+            wait(3)
+
+        @pl.when(jnp.logical_not(own_turn))
+        def _():
+            wait(4)
+
+        for j in range(4):
+            o = 4 * (q - low) + j
+            vector = all0[o].astype(F32)
+            for b in range(held):
+                row = jnp.concatenate([vector[b * blocks + c:b * blocks + c + 1] for c in range(blocks)], axis=1)
+                total = total + nt(spread(row), data_ref[:, columns(held * o + b)])
+        return total
+
+    ascent = lax.fori_loop(0, cubes - 2 * low, start_sum, jnp.zeros((ROWS, feats), F32))[0:1, :]
     scale = column_sq / samples + 1e-06
     stepped = w_start + ascent / (samples * scale)
     thresh = 1.0 / (4.0 * features * scale)
@@ -314,11 +383,24 @@
         orders.append(order)
         places.append(order.T.astype(BF16))
 
+    orders_half = [order.astype(BF16) for order in orders]
+    twice = [jnp.concatenate([place, place], axis=1) for place in places]
+
+    def upright(row, b):
+        piece = row[:, b * block:(b + 1) * block]
+        high = piece.astype(BF16).astype(F32)
+        both = jnp.broadcast_to(jnp.concatenate([high, piece - high], axis=1), (block, 2 * block))
+        return nt(twice[b], both.astype(BF16))
+
     alpha_zero = bound * frac_ref[...]
-
-    def permute(vectors):
-        stacked = jnp.concatenate(list(vectors) + [jnp.zeros((8 - len(vectors), rows), F32)], axis=0)
-        return [nn(stacked[:, b * block:(b + 1) * block], orders[b], HIGH) for b in range(blocks)]
+    for b in range(blocks):
+        sign_c[b] = upright(sign, b)
+        bound_c[b] = upright(bound, b)
+        alpha_c[b] = upright(alpha_zero, b)
+    pick_row = lax.broadcasted_iota(jnp.int32, (block, 2 * block), 0) % GROUP
+    pick_lane = lax.broadcasted_iota(jnp.int32, (block, 2 * block), 1) // block
+    for r in range(GROUP // 2):
+        picks[r] = (pick_row == pick_lane + 2 * r).astype(F32).astype(BF16)
 
     total_wait(got1, 1).wait_recv()
     received = jnp.sum(got1[...], axis=0)
@@ -326,62 +408,83 @@
     loss = jnp.sum(bound * jnp.square(jnp.maximum(0.0, 1.0 - sign * margin1)), axis=1, keepdims=True)
     penalty = jnp.sum(jnp.abs(primal), axis=1, keepdims=True)
     objective_part = loss / (2.0 * samples) + penalty / (4.0 * features)
-    permuted = permute((sign, bound, alpha_zero, diag, margin1))
-    sign_p = [x[0:1] for x in permuted]
-    bound_p = [x[1:2] for x in permuted]
-    zero_p = [x[2:3] for x in permuted]
-    inverse_p = [0.5 / (x[3:4] + 1e-06) for x in permuted]
-    margin_p = [x[4:5] for x in permuted]
-
-    view = gram_in.at[pl.ds(0, cubes - 1)]
-    gram_wait = pltpu.make_async_remote_copy(
-        src_ref=view, dst_ref=view, send_sem=gram_send.at[0], recv_sem=gram_recv.at[0],
-        device_id=(partner,), device_id_type=MESH,
-    )
-    gram_wait.wait_recv()
-    full = jnp.sum(gram_in[...].astype(F32), axis=0)
-    packed, cross = full[:, :block], full[:, block:]
+    inverse = 0.5 / (diag + 1e-06)
+    for b in range(blocks):
+        inverse_c[b] = upright(inverse, b)
+        margin_c[b] = upright(margin1, b)
+
+    wait_d(0).wait_recv()
+    packed = jnp.sum(gram_in[:, :, :block].astype(F32), axis=0)
     above, below = jnp.where(upper, packed, 0.0), jnp.where(lower, packed, 0.0)
-    blocks_p = {}
-    for (a, b), piece in {(0, 0): above + above.T, (0, 1): cross, (1, 1): below + below.T}.items():
-        piece = nn(piece.astype(BF16), orders[b].astype(BF16)).astype(BF16)
-        blocks_p[a, b] = nn(places[a], piece).astype(BF16)
-
-    lane = lax.broadcasted_iota(jnp.int32, (1, block), 1)
-    sub = lax.broadcasted_iota(jnp.int32, (ROWS, block), 0)
-
-    def times_gram(delta, piece):
-        high = delta.astype(BF16).astype(F32)
-        lhs = jnp.where(sub == 0, high, jnp.where(sub == 1, delta - high, 0.0)).astype(BF16)
-        return 2.0 * jnp.sum(nn(lhs, piece)[0:8], axis=0, keepdims=True)
-
-    def sweep(alpha, margin):
-        result, margin = [], list(margin)
+    gap = row_at // GROUP - lane_at // GROUP
+
+    def visited(a, b, piece):
+        piece = nn(piece.astype(BF16), orders_half[b]).astype(BF16)
+        return nn(places[a], piece)
+
+    for b, piece in enumerate((above + above.T, below + below.T)):
+        whole = visited(b, b, piece)
+        square[b] = whole
+        lagged = [jnp.where(gap == lag, whole, 0.0)[lag * GROUP:] for lag in (1, 2)]
+        lagged = jnp.concatenate(lagged, axis=0).astype(BF16)
+        for r in range(GROUP // 2):
+            spots = nn(lagged, picks[r])
+            for c in range(2):
+                half = spots[:, c * block:(c + 1) * block]
+                table[0, b, 2 * r + c, GROUP:, :] = half[:block - GROUP]
+                table[1, b, 2 * r + c, 2 * GROUP:, :] = half[block - GROUP:]
+    wait_d(1).wait_recv()
+    between = visited(0, 1, jnp.sum(gram_in[:, :, block:].astype(F32), axis=0))
+    sub = lax.broadcasted_iota(jnp.int32, (GROUP, block), 0)
+    lane = lax.broadcasted_iota(jnp.int32, (GROUP, block), 1)
+
+    def fold(x):
+        return x[0:8] + x[8:16]
+
+    def total_of(terms):
+        while len(terms) > 1:
+            terms = [sum(terms[i:i + 2]) for i in range(0, len(terms), 2)]
+        return terms[0]
+
+    def sweep():
+        sets, offset, moves = block // GROUP, None, []
         for b in range(blocks):
-            now, m, moved = alpha[b], margin[b], jnp.zeros((1, block), F32)
-            for s in range(block // GROUP):
-                fresh = jnp.clip(now + (1.0 - sign_p[b] * m) * inverse_p[b], 0.0, bound_p[b])
-                mine = (lane >= s * GROUP) & (lane < (s + 1) * GROUP)
-                change = jnp.where(mine, fresh - now, 0.0)
-                now = jnp.where(mine, fresh, now)
-                change = sign_p[b] * change
-                moved = moved + change
-                if s + 1 < block // GROUP:
-                    m = m + times_gram(change, blocks_p[b, b])
-            for later in range(b + 1, blocks):
-                margin[later] = margin[later] + times_gram(moved, blocks_p[b, later])
-            result.append(now)
-        return result
-
-    def changes(after, before):
-        pieces = []
-        for b in range(blocks):
-            z = spread(sign_p[b] * (after[b] - before[b]))
-            pieces.append(nt(z, orders[b].astype(BF16))[0:1, :])
-        return jnp.concatenate(pieces, axis=1)
-
-    one_p = sweep(zero_p, margin_p)
-    own1[0:1, 0:rows] = changes(one_p, zero_p)
+            seen, passed, moved = [jnp.zeros((8, block), F32) for _ in range(3)]
+            extra = [[] for _ in range(sets)]
+            for s in range(sets):
+                at = slice(s * GROUP, (s + 1) * GROUP)
+                m = margin_c[b, at]
+                if offset is not None:
+                    m = m + offset[at]
+                for term in extra[s]:
+                    m = m + term
+                now, side = alpha_c[b, at], sign_c[b, at]
+                fresh = jnp.clip(now + (1.0 - side * m) * inverse_c[b, at], 0.0, bound_c[b, at])
+                change = side * (fresh - now)
+                alpha_c[b, at] = fresh
+                moved = moved + fold(jnp.where(lane == sub + s * GROUP, change, 0.0))
+                push = 2.0 * change
+                steps = [jnp.broadcast_to(push[r:r + 1], (GROUP, block)) for r in range(GROUP)]
+                if s + 3 < sets:
+                    seen = seen + fold(push * square[b, at])
+                    row = jnp.sum(seen, axis=0, keepdims=True)
+                    spot = jnp.where(lane == sub + (s + 3) * GROUP, row, 0.0)
+                    extra[s + 3].append(jnp.sum(spot, axis=1, keepdims=True))
+                for lag in (2, 1):
+                    if s + lag < sets:
+                        there = slice((s + lag) * GROUP, (s + lag + 1) * GROUP)
+                        extra[s + lag].append(
+                            total_of([steps[r] * table[lag - 1, b, r, there] for r in range(GROUP)])
+                        )
+                if b + 1 < blocks:
+                    passed = passed + fold(push * between[at])
+            moves.append(jnp.sum(moved, axis=0, keepdims=True))
+            if b + 1 < blocks:
+                row = jnp.sum(passed, axis=0, keepdims=True)
+                offset = jnp.sum(jnp.where(even, row, 0.0), axis=1, keepdims=True)
+        return jnp.concatenate([nt(spread(x), orders_half[b])[0:1, :] for b, x in enumerate(moves)], axis=1)
+
+    own1[0:1, 0:rows] = sweep()
     own1[0:1, rows:] = jnp.broadcast_to(objective_part, (1, block))
     gather_start(own1, all1, 1 + 3)
     update_one = back(all1, 4) * (2.0 / devices)
@@ -389,22 +492,34 @@
     out_ref[:, feats + rows:] = jnp.sum(all1[...], axis=0)[:, rows:]
     total_wait(got2, 2).wait_recv()
     margin2 = margin1 + jnp.sum(got2[...], axis=0)
-    margin2_p = [x[0:1] for x in permute((margin2,))]
-    two_p = sweep(one_p, margin2_p)
-    own2[...] = changes(two_p, one_p)
+    for b in range(blocks):
+        margin_c[b] = upright(margin2, b)
+    own2[...] = sweep()
     gather_start(own2, all2, 2 + 3)
     def alpha_out():
         for b in range(blocks):
-            spot = jnp.broadcast_to(two_p[b], (8, block))
+            spot = jnp.broadcast_to(jnp.sum(jnp.where(even, alpha_c[b], 0.0), axis=0, keepdims=True), (8, block))
             out_ref[:, feats + b * block:feats + (b + 1) * block] = nt(spot, orders[b], HIGH)[0:1, :]
 
     out_ref[:, :feats] = primal + update_one + back(all2, 5, alpha_out) * (2.0 / devices)
 
-    for phase, ref in enumerate((got0, got1, got2)):
+    for phase, ref in ((1, got1), (2, got2), (4, all1), (5, all2)):
         total_wait(ref, phase).wait_send()
-    for phase, ref in enumerate((all0, all1, all2)):
-        total_wait(ref, phase + 3).wait_send()
-    gram_wait.wait_send()
+
+    @pl.when(is_owner)
+    def _():
+        waiting(part0, owners - 1, send_sem.at[0], recv_sem.at[0]).wait_send()
+        def sent(_):
+            remote(own0, all0.at[0], send_sem.at[3], recv_sem.at[0], partner).wait_send()
+
+        loop(0, devices - 1, sent)
+
+    @pl.when(jnp.logical_not(is_owner))
+    def _():
+        waiting(part0, owners, send_sem.at[0], recv_sem.at[0]).wait_send()
+
+    wait_d(0).wait_send()
+    wait_d(1).wait_send()
 
     def drain(i):
         for j in range(4):
@@ -428,6 +543,9 @@
     rows = alpha_start.shape[0]
     blocks, block = visit_order.shape
     cubes = devices // 8
+    owners = cubes // 2 * 4
+    span = (devices // owners * blocks, block)
+    tiles = [x.reshape(owners, *span) for x in (labels, sample_weight)]
     labels = labels.reshape(devices, 1, rows)
     bound = sample_weight.reshape(devices, 1, rows)
 
@@ -445,25 +563,28 @@
         functools.partial(kernel, devices),
         name="svm_rounds",
         out_shape=jax.ShapeDtypeStruct((1, feats + rows + block), F32),
-        in_specs=[pl.BlockSpec(memory_space=pl.ANY)] * 6,
+        in_specs=[pl.BlockSpec(memory_space=pl.ANY)] * 8,
         out_specs=vmem,
         scratch_shapes=[
-            vectors(1, rows), vectors(2, rows), vectors(1, rows),
-            vectors(1, rows), vectors(2, rows), vectors(1, rows),
-            pltpu.VMEM((1, rows), F32), pltpu.VMEM((1, rows + block), F32), pltpu.VMEM((1, rows), F32),
-            vectors(1, rows), vectors(1, rows + block), vectors(1, rows),
+            pltpu.VMEM((owners, *span), F32), vectors(2, rows), vectors(1, rows),
+            pltpu.VMEM((devices, *span), F32), vectors(2, rows), vectors(1, rows),
+            pltpu.VMEM(span, BF16), pltpu.VMEM((1, rows + block), F32), pltpu.VMEM((1, rows), F32),
+            pltpu.VMEM((owners, *span), BF16), vectors(1, rows + block), vectors(1, rows),
             pltpu.VMEM(data_t.shape, BF16), pltpu.VMEM((1, rows), jnp.int32), pltpu.VMEM((1, rows), F32),
+            pltpu.VMEM(span, jnp.int32), pltpu.VMEM(span, F32),
             pltpu.VMEM((1, feats), F32), pltpu.VMEM((1, rows), F32), pltpu.VMEM((blocks, block), jnp.int32),
             pltpu.VMEM((feats, block), F32), grams(devices), grams(4 * cubes), grams(2 * cubes), grams(cubes),
             grams(4 * cubes), grams(2 * cubes), grams(cubes), grams(cubes),
-            semaphores(cubes), semaphores(5), semaphores(6), semaphores(3), semaphores(3 * cubes), semaphores(4 * cubes), semaphores(4 * cubes),
+            pltpu.VMEM((GROUP // 2, block, 2 * block), BF16), pltpu.VMEM((2, blocks, GROUP, block, block), F32),
+            *[pltpu.VMEM((blocks, block, block), F32)] * 6,
+            semaphores(cubes), semaphores(7), semaphores(6), semaphores(3), semaphores(3 * cubes), semaphores(4 * cubes), semaphores(4 * cubes),
             semaphores(2 * cubes), semaphores(2 * cubes), semaphores(cubes), semaphores(cubes),
-            semaphores(1), semaphores(1),
+            semaphores(2), semaphores(2),
         ],
         compiler_params=pltpu.CompilerParams(
             collective_id=0, has_side_effects=True, vmem_limit_bytes=63 * 1024 * 1024
         ),
-    )(data_t, labels, bound, w_start[None], alpha_start[None], visit_order)
+    )(data_t, labels, bound, *tiles, w_start[None], alpha_start[None], visit_order)
     weights, alpha, objective = pl.pallas_call(
         split,
         name="split",

time: 48.7 us -> 45.1 us (0.926)
  Pallas kernels: 47.9 us -> 44.2 us
    pallas_call x1, Pallas kernels: 46.7 us -> 43 us  [body(): pl.pallas_call(functools.partial(kernel, devices), name='svm_rounds', out...]
where the time goes in v2:
time: 45.1 us; the launch traced here: 44.9 us
  Pallas kernels  44.2 us (98%)
  between operations  0.64 us (1%)
    pallas_call x1, Pallas kernels, body(): pl.pallas_call(functools.partial(kernel, devices), name='svm_rounds', out...  43 us
    pallas_call x1, Pallas kernels, body(): pl.pallas_call(split, name='split', out_shape=(jax.ShapeDtypeStruct((1, f...  1.24 us

profile of v2, /device:TPU:0, one launch (start us, length us, event | category | flops | bytes accessed | tf_op | source)
XLA Modules:
  0.0 44.9 jit_solution(1205081938413844755)
XLA Ops:
  0.6 43.0 %svm_rounds.1.packed = f32[1,640]{1,0:T(1,128)} custom-call(bf16[256,8192]{1,0:T(8,128)(2,1)} %data_hbm.1, s32[32,1,256]{2,1,0:T(1,128)} %bitcast.9, f32[32,1,256]{2,1,0:T(1,128)} %bitcast.11, s32[8,8,128]{2,1,0:T(8,128)} %bitcast.10, f32[8,8,128]{2,1,0:T(8,128)} %bitcast.12, f32[1,256]{1,0:T(1,128)} %bitcast.13, f32[1,256]{1,0:T(1,128)} %bitcast.14, ...), custom_call_target="tpu_custom_call" | custom-call | tf_op jit(solution)/shard_map/svm_rounds/pallas_call | solution.py:562
  43.6 1.2 %split.1 = (f32[1,256]{1,0:T(1,128)}, f32[1,256]{1,0:T(1,128)}, f32[1,1]{1,0:T(1,128)}) custom-call(f32[1,640]{1,0:T(1,128)} %svm_rounds.1.packed), custom_call_target="tpu_custom_call" | custom-call | tf_op jit(solution)/shard_map/split/pallas_call | solution.py:588

commit v3 on v2

--- a/solution.py
+++ b/solution.py
@@ -30,9 +30,9 @@
 def kernel(
     devices, data_hbm, label_hbm, bound_hbm, label_tiles, bound_tiles, start_hbm, frac_hbm, visit_hbm,
     out_ref,
-    part0, part1, part2, got0, got1, got2, own0, own1, own2, all0, all1, all2,
-    data_ref, label_ref, bound_ref, owned_label, owned_bound, start_ref, frac_ref, visit_ref, squares, gram, in_a, in_b, in_c, sum_a, sum_b, sum_c, gram_in,
-    picks, table, square, sign_c, bound_c, inverse_c, alpha_c, margin_c,
+    part0, part1, part2, part_d, got0, got1, got2, got_d, own0, own1, own2, own_o, all0, all1, all2, all_o,
+    data_ref, turned_ref, label_ref, bound_ref, owned_label, owned_bound, start_ref, frac_ref, visit_ref, squares, gram, in_a, in_b, in_c, sum_a, sum_b, sum_c, gram_in,
+    picks, table, between_c, square, sign_c, bound_c, inverse_c, alpha_c, margin_c,
     load_sem, small_sem, send_sem, recv_sem, gather_sem, send_a, recv_a, send_b, recv_b, send_c, recv_c, gram_send, gram_recv,
 ):
     me = lax.axis_index("shard")
@@ -87,11 +87,12 @@
 
     def total_wait(ref, phase):
         view = ref.at[pl.ds(0, devices - 1)]
-        return remote(view, view, send_sem.at[phase], recv_sem.at[phase % 3], partner)
+        return remote(view, view, send_sem.at[phase], recv_sem.at[phase % 3 if phase < 6 else phase - 3], partner)
 
     def scatter_send(part, got, phase):
         def send(peer):
-            remote(part.at[peer], got.at[me], send_sem.at[phase], recv_sem.at[phase], peer).start()
+            arrived = recv_sem.at[phase if phase < 3 else phase - 3]
+            remote(part.at[peer], got.at[me], send_sem.at[phase], arrived, peer).start()
 
         return send
 
@@ -128,7 +129,9 @@
         def cube_sum(q, total):
             for j in range(8):
                 k = 8 * q + j
-                total = total + nt(spread(everyone[k][0:1, 0:rows]), data_ref[:, columns(k)])
+                vector = everyone[k].astype(F32)
+                row = jnp.concatenate([vector[b:b + 1] for b in range(blocks)], axis=1)
+                total = total + nn(spread(row), turned_ref[k])
             return total
 
         def step(i, total):
@@ -169,48 +172,49 @@
     def gram_of(k):
         tile = data_ref[:, columns(k)]
         first, second = tile[:, :block], tile[:, block:]
-        top = lax.dot_general(first, tile, (((0,), (0,)), ((), ())), preferred_element_type=F32)
-        low = lax.dot_general(second, second, (((0,), (0,)), ((), ())), preferred_element_type=F32)
-        gram[k, :, :block] = jnp.where(upper, top[:, :block], low).astype(BF16)
-        gram[k, :, block:] = top[:, block:].astype(BF16)
-        part1[k, 1:2, :block] = jnp.sum(jnp.where(even, top[:, :block], 0.0), axis=0, keepdims=True)
-        part1[k, 1:2, block:] = jnp.sum(jnp.where(even, low, 0.0), axis=0, keepdims=True)
+        turned = tile.T
+        turned_ref[k] = turned
+        top, low = nn(turned[:block], tile), nn(turned[block:], second)
+        gram[k, 0] = jnp.where(upper, top[:, :block], low).astype(BF16)
+        gram[k, 1] = top[:, block:].astype(BF16)
+        part_d[k, 0:1, :block] = jnp.sum(jnp.where(even, top[:, :block], 0.0), axis=0, keepdims=True)
+        part_d[k, 0:1, block:] = jnp.sum(jnp.where(even, low, 0.0), axis=0, keepdims=True)
 
     def halving(source, target, index, sends, recvs, peer):
         return pltpu.make_async_remote_copy(
-            src_ref=source, dst_ref=target.at[index], send_sem=sends.at[index],
+            src_ref=source, dst_ref=target, send_sem=sends.at[index],
             recv_sem=recvs.at[index], device_id=(peer,), device_id_type=MESH,
         )
 
     def copy_a(q, j):
-        return halving(gram.at[8 * q + 2 * j + 1 - bit0], in_a, 4 * q + j, send_a, recv_a, partner)
-
-    def order_of(i):
-        swap = i % 2
-        return (1 - swap) * bit1 + swap * bit2, 1 + swap, (1 - swap) * bit2 + swap * bit1, 2 - swap
-
-    def copy_b(i, t):
+        return halving(gram.at[8 * q + 2 * j + 1 - bit0], in_a.at[4 * q + j], 4 * q + j, send_a, recv_a, partner)
+
+    orders_of = ((bit1, 1, bit2, 2), (bit2, 2, bit1, 1))
+
+    def copy_b(i, t, half):
         q = turn(i)
-        bit, weight, _, other = order_of(i)
+        bit, weight, _, other = orders_of[half]
         return halving(
-            sum_a.at[4 * q + weight * (1 - bit) + other * t], in_b, 2 * q + t, send_b, recv_b,
-            me + 2 * weight * (1 - 2 * bit),
+            sum_a.at[4 * q + weight * (1 - bit) + other * t, half], in_b.at[2 * q + t, half],
+            4 * q + 2 * t + half, send_b, recv_b, me + 2 * weight * (1 - 2 * bit),
         )
 
-    def copy_c(i):
+    def copy_c(i, half):
         q = turn(i)
-        _, _, bit, weight = order_of(i)
-        return halving(sum_b.at[2 * q + 1 - bit], in_c, q, send_c, recv_c, me + 2 * weight * (1 - 2 * bit))
+        _, _, bit, weight = orders_of[half]
+        return halving(
+            sum_b.at[2 * q + 1 - bit, half], in_c.at[q, half],
+            2 * q + half, send_c, recv_c, me + 2 * weight * (1 - 2 * bit),
+        )
 
     def copy_d(q, half):
-        view = pl.ds(half * block, block)
         return pltpu.make_async_remote_copy(
-            src_ref=sum_c.at[q, :, view], dst_ref=gram_in.at[cube, :, view], send_sem=gram_send.at[half],
+            src_ref=sum_c.at[q, half], dst_ref=gram_in.at[cube, half], send_sem=gram_send.at[half],
             recv_sem=gram_recv.at[half], device_id=(me + 8 * (q - cube),), device_id_type=MESH,
         )
 
     def wait_d(half):
-        view = gram_in.at[pl.ds(0, cubes - 1), :, pl.ds(half * block, block)]
+        view = gram_in.at[pl.ds(0, cubes - 1), half]
         return pltpu.make_async_remote_copy(
             src_ref=view, dst_ref=view, send_sem=gram_send.at[half], recv_sem=gram_recv.at[half],
             device_id=(partner,), device_id_type=MESH,
@@ -224,33 +228,37 @@
 
     def merge_a(i):
         q = turn(i)
-        bit, weight, last, other = order_of(i)
-        for t in (1 - last, last):
-            for side in (1 - bit, bit):
-                at = weight * side + other * t
-                copy_a(q, at).wait_recv()
-                sum_a[4 * q + at] = added(gram[8 * q + 2 * at + bit0], in_a[4 * q + at])
-            copy_b(i, t).start()
+        for j in range(4):
+            copy_a(q, j).wait_recv()
+            sum_a[4 * q + j] = added(gram[8 * q + 2 * j + bit0], in_a[4 * q + j])
+        for half in range(2):
+            for t in (1 - orders_of[half][2], orders_of[half][2]):
+                copy_b(i, t, half).start()
 
     def merge_b(i):
         q = turn(i)
-        bit, weight, last, other = order_of(i)
-        for t in (1 - last, last):
-            copy_b(i, t).wait_recv()
-            sum_b[2 * q + t] = added(sum_a[4 * q + weight * bit + other * t], in_b[2 * q + t])
-        copy_c(i).start()
-
-    def merged_c(i):
+        for half in range(2):
+            bit, weight, last, other = orders_of[half]
+            for t in (1 - last, last):
+                copy_b(i, t, half).wait_recv()
+                sum_b[2 * q + t, half] = added(
+                    sum_a[4 * q + weight * bit + other * t, half], in_b[2 * q + t, half]
+                )
+            copy_c(i, half).start()
+
+    def merged_c(i, half):
         q = turn(i)
-        bit = order_of(i)[2]
-        copy_c(i).wait_recv()
-        return added(sum_b[2 * q + bit], in_c[q])
+        copy_c(i, half).wait_recv()
+        return added(sum_b[2 * q + orders_of[half][2], half], in_c[q, half])
 
     def merge_c(i):
         q = turn(i)
-        sum_c[q] = merged_c(i)
+        for half in range(2):
+            sum_c[q, half] = merged_c(i, half)
         copy_d(q, 0).start()
-        copy_d(q, 1).start()
+
+    def merge_x(i):
+        copy_d(turn(i), 1).start()
 
     def start_a(i):
         for j in range(4):
@@ -335,6 +343,8 @@
         all0[mine] = own0[...]
         peers(lambda peer: remote(own0, all0.at[mine], send_sem.at[3], gather_sem.at[cube], peer).start())
 
+    peers(scatter_send(part_d, got_d, 6))
+    got_d[me] = part_d[me]
     merge_a(cubes - 2)
     loop(0, cubes - 2, merge_b)
     merge_a(cubes - 1)
@@ -362,7 +372,7 @@
             vector = all0[o].astype(F32)
             for b in range(held):
                 row = jnp.concatenate([vector[b * blocks + c:b * blocks + c + 1] for c in range(blocks)], axis=1)
-                total = total + nt(spread(row), data_ref[:, columns(held * o + b)])
+                total = total + nn(spread(row), turned_ref[held * o + b])
         return total
 
     ascent = lax.fori_loop(0, cubes - 2 * low, start_sum, jnp.zeros((ROWS, feats), F32))[0:1, :]
@@ -373,9 +383,18 @@
     margin_scatter(primal, part1, got1, 1)
     merge_b(cubes - 2)
     merge_c(0)
+
+    def middle_step(i):
+        merge_c(i)
+        merge_x(i - 1)
+
+    loop(1, cubes - 2, middle_step)
     merge_b(cubes - 1)
-    loop(1, cubes - 1, merge_c)
-    gram_in[cube] = merged_c(cubes - 1)
+    merge_c(cubes - 2)
+    merge_x(cubes - 3)
+    merge_x(cubes - 2)
+    for half in range(2):
+        gram_in[cube, half] = merged_c(cubes - 1, half)
 
     orders, places = [], []
     for b in range(blocks):
@@ -403,8 +422,8 @@
         picks[r] = (pick_row == pick_lane + 2 * r).astype(F32).astype(BF16)
 
     total_wait(got1, 1).wait_recv()
-    received = jnp.sum(got1[...], axis=0)
-    margin1, diag = received[0:1, :], received[1:2, :]
+    total_wait(got_d, 6).wait_recv()
+    margin1, diag = jnp.sum(got1[...], axis=0), jnp.sum(got_d[...], axis=0)
     loss = jnp.sum(bound * jnp.square(jnp.maximum(0.0, 1.0 - sign * margin1)), axis=1, keepdims=True)
     penalty = jnp.sum(jnp.abs(primal), axis=1, keepdims=True)
     objective_part = loss / (2.0 * samples) + penalty / (4.0 * features)
@@ -414,7 +433,7 @@
         margin_c[b] = upright(margin1, b)
 
     wait_d(0).wait_recv()
-    packed = jnp.sum(gram_in[:, :, :block].astype(F32), axis=0)
+    packed = jnp.sum(gram_in[:, 0].astype(F32), axis=0)
     above, below = jnp.where(upper, packed, 0.0), jnp.where(lower, packed, 0.0)
     gap = row_at // GROUP - lane_at // GROUP
 
@@ -433,8 +452,6 @@
                 half = spots[:, c * block:(c + 1) * block]
                 table[0, b, 2 * r + c, GROUP:, :] = half[:block - GROUP]
                 table[1, b, 2 * r + c, 2 * GROUP:, :] = half[block - GROUP:]
-    wait_d(1).wait_recv()
-    between = visited(0, 1, jnp.sum(gram_in[:, :, block:].astype(F32), axis=0))
     sub = lax.broadcasted_iota(jnp.int32, (GROUP, block), 0)
     lane = lax.broadcasted_iota(jnp.int32, (GROUP, block), 1)
 
@@ -446,55 +463,64 @@
             terms = [sum(terms[i:i + 2]) for i in range(0, len(terms), 2)]
         return terms[0]
 
-    def sweep():
-        sets, offset, moves = block // GROUP, None, []
-        for b in range(blocks):
-            seen, passed, moved = [jnp.zeros((8, block), F32) for _ in range(3)]
-            extra = [[] for _ in range(sets)]
-            for s in range(sets):
-                at = slice(s * GROUP, (s + 1) * GROUP)
-                m = margin_c[b, at]
-                if offset is not None:
-                    m = m + offset[at]
-                for term in extra[s]:
-                    m = m + term
-                now, side = alpha_c[b, at], sign_c[b, at]
-                fresh = jnp.clip(now + (1.0 - side * m) * inverse_c[b, at], 0.0, bound_c[b, at])
-                change = side * (fresh - now)
-                alpha_c[b, at] = fresh
-                moved = moved + fold(jnp.where(lane == sub + s * GROUP, change, 0.0))
-                push = 2.0 * change
-                steps = [jnp.broadcast_to(push[r:r + 1], (GROUP, block)) for r in range(GROUP)]
-                if s + 3 < sets:
-                    seen = seen + fold(push * square[b, at])
-                    row = jnp.sum(seen, axis=0, keepdims=True)
-                    spot = jnp.where(lane == sub + (s + 3) * GROUP, row, 0.0)
-                    extra[s + 3].append(jnp.sum(spot, axis=1, keepdims=True))
-                for lag in (2, 1):
-                    if s + lag < sets:
-                        there = slice((s + lag) * GROUP, (s + lag + 1) * GROUP)
-                        extra[s + lag].append(
-                            total_of([steps[r] * table[lag - 1, b, r, there] for r in range(GROUP)])
-                        )
-                if b + 1 < blocks:
-                    passed = passed + fold(push * between[at])
-            moves.append(jnp.sum(moved, axis=0, keepdims=True))
-            if b + 1 < blocks:
-                row = jnp.sum(passed, axis=0, keepdims=True)
-                offset = jnp.sum(jnp.where(even, row, 0.0), axis=1, keepdims=True)
-        return jnp.concatenate([nt(spread(x), orders_half[b])[0:1, :] for b, x in enumerate(moves)], axis=1)
-
-    own1[0:1, 0:rows] = sweep()
-    own1[0:1, rows:] = jnp.broadcast_to(objective_part, (1, block))
+    def sweep_block(b, offset):
+        sets = block // GROUP
+        seen, moved, pushes = jnp.zeros((8, block), F32), jnp.zeros((8, block), F32), []
+        extra = [[] for _ in range(sets)]
+        for s in range(sets):
+            at = slice(s * GROUP, (s + 1) * GROUP)
+            m = margin_c[b, at]
+            if offset is not None:
+                m = m + offset[at]
+            for term in extra[s]:
+                m = m + term
+            now, side = alpha_c[b, at], sign_c[b, at]
+            fresh = jnp.clip(now + (1.0 - side * m) * inverse_c[b, at], 0.0, bound_c[b, at])
+            change = side * (fresh - now)
+            alpha_c[b, at] = fresh
+            moved = moved + fold(jnp.where(lane == sub + s * GROUP, change, 0.0))
+            push = 2.0 * change
+            pushes.append(push)
+            steps = [jnp.broadcast_to(push[r:r + 1], (GROUP, block)) for r in range(GROUP)]
+            if s + 3 < sets:
+                seen = seen + fold(push * square[b, at])
+                row = jnp.sum(seen, axis=0, keepdims=True)
+                spot = jnp.where(lane == sub + (s + 3) * GROUP, row, 0.0)
+                extra[s + 3].append(jnp.sum(spot, axis=1, keepdims=True))
+            for lag in (2, 1):
+                if s + lag < sets:
+                    there = slice((s + lag) * GROUP, (s + lag + 1) * GROUP)
+                    extra[s + lag].append(
+                        total_of([steps[r] * table[lag - 1, b, r, there] for r in range(GROUP)])
+                    )
+        line = jnp.sum(moved, axis=0, keepdims=True)
+        return nt(spread(line), orders_half[b])[0:1, :], pushes
+
+    def passed_on(pushes):
+        terms = [fold(push * between_c[s * GROUP:(s + 1) * GROUP]) for s, push in enumerate(pushes)]
+        row = jnp.sum(total_of(terms), axis=0, keepdims=True)
+        return jnp.sum(jnp.where(even, row, 0.0), axis=1, keepdims=True)
+
+    first, pushes = sweep_block(0, None)
+    wait_d(1).wait_recv()
+    between_c[...] = visited(0, 1, jnp.sum(gram_in[:, 1].astype(F32), axis=0))
+    second, _ = sweep_block(1, passed_on(pushes))
+    own1[...] = jnp.concatenate([first, second], axis=0).astype(BF16)
+    own_o[...] = jnp.broadcast_to(objective_part, (1, block))
+    all_o[me] = own_o[...]
     gather_start(own1, all1, 1 + 3)
+    peers(lambda peer: remote(own_o, all_o.at[me], send_sem.at[7], recv_sem.at[4], peer).start())
     update_one = back(all1, 4) * (2.0 / devices)
     margin_scatter(update_one, part2, got2, 2)
-    out_ref[:, feats + rows:] = jnp.sum(all1[...], axis=0)[:, rows:]
+    total_wait(all_o, 7).wait_recv()
+    out_ref[:, feats + rows:] = jnp.sum(all_o[...], axis=0)
     total_wait(got2, 2).wait_recv()
     margin2 = margin1 + jnp.sum(got2[...], axis=0)
     for b in range(blocks):
         margin_c[b] = upright(margin2, b)
-    own2[...] = sweep()
+    first, pushes = sweep_block(0, None)
+    second, _ = sweep_block(1, passed_on(pushes))
+    own2[...] = jnp.concatenate([first, second], axis=0).astype(BF16)
     gather_start(own2, all2, 2 + 3)
     def alpha_out():
         for b in range(blocks):
@@ -503,7 +529,7 @@
 
     out_ref[:, :feats] = primal + update_one + back(all2, 5, alpha_out) * (2.0 / devices)
 
-    for phase, ref in ((1, got1), (2, got2), (4, all1), (5, all2)):
+    for phase, ref in ((1, got1), (2, got2), (4, all1), (5, all2), (6, got_d), (7, all_o)):
         total_wait(ref, phase).wait_send()
 
     @pl.when(is_owner)
@@ -524,9 +550,10 @@
     def drain(i):
         for j in range(4):
             copy_a(turn(i), j).wait_send()
-        for j in range(2):
-            copy_b(i, j).wait_send()
-        copy_c(i).wait_send()
+        for half in range(2):
+            for j in range(2):
+                copy_b(i, j, half).wait_send()
+            copy_c(i, half).wait_send()
 
     loop(0, cubes, drain)
 
@@ -550,7 +577,7 @@
     bound = sample_weight.reshape(devices, 1, rows)
 
     def grams(count):
-        return pltpu.VMEM((count, block, rows), BF16)
+        return pltpu.VMEM((count, rows // block, block, block), BF16)
 
     def semaphores(count):
         return pltpu.SemaphoreType.DMA((count,))
@@ -566,19 +593,20 @@
         in_specs=[pl.BlockSpec(memory_space=pl.ANY)] * 8,
         out_specs=vmem,
         scratch_shapes=[
-            pltpu.VMEM((owners, *span), F32), vectors(2, rows), vectors(1, rows),
-            pltpu.VMEM((devices, *span), F32), vectors(2, rows), vectors(1, rows),
-            pltpu.VMEM(span, BF16), pltpu.VMEM((1, rows + block), F32), pltpu.VMEM((1, rows), F32),
-            pltpu.VMEM((owners, *span), BF16), vectors(1, rows + block), vectors(1, rows),
-            pltpu.VMEM(data_t.shape, BF16), pltpu.VMEM((1, rows), jnp.int32), pltpu.VMEM((1, rows), F32),
+            pltpu.VMEM((owners, *span), F32), vectors(1, rows), vectors(1, rows), vectors(1, rows),
+            pltpu.VMEM((devices, *span), F32), vectors(1, rows), vectors(1, rows), vectors(1, rows),
+            pltpu.VMEM(span, BF16), pltpu.VMEM((blocks, block), BF16), pltpu.VMEM((blocks, block), BF16),
+            pltpu.VMEM((1, block), F32), pltpu.VMEM((owners, *span), BF16),
+            *[pltpu.VMEM((devices, blocks, block), BF16)] * 2, vectors(1, block),
+            pltpu.VMEM(data_t.shape, BF16), pltpu.VMEM((devices, rows, feats), BF16), pltpu.VMEM((1, rows), jnp.int32), pltpu.VMEM((1, rows), F32),
             pltpu.VMEM(span, jnp.int32), pltpu.VMEM(span, F32),
             pltpu.VMEM((1, feats), F32), pltpu.VMEM((1, rows), F32), pltpu.VMEM((blocks, block), jnp.int32),
             pltpu.VMEM((feats, block), F32), grams(devices), grams(4 * cubes), grams(2 * cubes), grams(cubes),
             grams(4 * cubes), grams(2 * cubes), grams(cubes), grams(cubes),
             pltpu.VMEM((GROUP // 2, block, 2 * block), BF16), pltpu.VMEM((2, blocks, GROUP, block, block), F32),
-            *[pltpu.VMEM((blocks, block, block), F32)] * 6,
-            semaphores(cubes), semaphores(7), semaphores(6), semaphores(3), semaphores(3 * cubes), semaphores(4 * cubes), semaphores(4 * cubes),
-            semaphores(2 * cubes), semaphores(2 * cubes), semaphores(cubes), semaphores(cubes),
+            pltpu.VMEM((block, block), F32), *[pltpu.VMEM((blocks, block, block), F32)] * 6,
+            semaphores(cubes), semaphores(7), semaphores(8), semaphores(5), semaphores(3 * cubes), semaphores(4 * cubes), semaphores(4 * cubes),
+            semaphores(4 * cubes), semaphores(4 * cubes), semaphores(2 * cubes), semaphores(2 * cubes),
             semaphores(2), semaphores(2),
         ],
         compiler_params=pltpu.CompilerParams(

time: 45.1 us -> 43.5 us (0.965)
  Pallas kernels: 44.2 us -> 42.7 us
    pallas_call x1, Pallas kernels: 43 us -> 41.4 us  [body(): pl.pallas_call(functools.partial(kernel, devices), name='svm_rounds', out...]
where the time goes in v3:
time: 43.5 us; the launch traced here: 43.3 us
  Pallas kernels  42.7 us (98%)
  between operations  0.64 us (1%)
    pallas_call x1, Pallas kernels, body(): pl.pallas_call(functools.partial(kernel, devices), name='svm_rounds', out...  41.4 us
    pallas_call x1, Pallas kernels, body(): pl.pallas_call(split, name='split', out_shape=(jax.ShapeDtypeStruct((1, f...  1.24 us

profile of v3, /device:TPU:0, one launch (start us, length us, event | category | flops | bytes accessed | tf_op | source)
XLA Modules:
  0.0 43.3 jit_solution(7215202392086931571)
XLA Ops:
  0.6 41.4 %svm_rounds.1.packed = f32[1,640]{1,0:T(1,128)} custom-call(bf16[256,8192]{1,0:T(8,128)(2,1)} %data_hbm.1, s32[32,1,256]{2,1,0:T(1,128)} %bitcast.9, f32[32,1,256]{2,1,0:T(1,128)} %bitcast.11, s32[8,8,128]{2,1,0:T(8,128)} %bitcast.10, f32[8,8,128]{2,1,0:T(8,128)} %bitcast.12, f32[1,256]{1,0:T(1,128)} %bitcast.13, f32[1,256]{1,0:T(1,128)} %bitcast.14, ...), custom_call_target="tpu_custom_call" | custom-call | tf_op jit(solution)/shard_map/svm_rounds/pallas_call | solution.py:589
  42.1 1.2 %split.1 = (f32[1,256]{1,0:T(1,128)}, f32[1,256]{1,0:T(1,128)}, f32[1,1]{1,0:T(1,128)}) custom-call(f32[1,640]{1,0:T(1,128)} %svm_rounds.1.packed), custom_call_target="tpu_custom_call" | custom-call | tf_op jit(solution)/shard_map/split/pallas_call | solution.py:616

commit v4 on v3

--- a/solution.py
+++ b/solution.py
@@ -182,12 +182,12 @@
 
     def halving(source, target, index, sends, recvs, peer):
         return pltpu.make_async_remote_copy(
-            src_ref=source, dst_ref=target, send_sem=sends.at[index],
+            src_ref=source, dst_ref=target, send_sem=sends.at[0],
             recv_sem=recvs.at[index], device_id=(peer,), device_id_type=MESH,
         )
 
     def copy_a(q, j):
-        return halving(gram.at[8 * q + 2 * j + 1 - bit0], in_a.at[4 * q + j], 4 * q + j, send_a, recv_a, partner)
+        return halving(gram.at[8 * q + 2 * j + 1 - bit0], in_a.at[4 * q + j], q, send_a, recv_a, partner)
 
     orders_of = ((bit1, 1, bit2, 2), (bit2, 2, bit1, 1))
 
@@ -196,7 +196,7 @@
         bit, weight, _, other = orders_of[half]
         return halving(
             sum_a.at[4 * q + weight * (1 - bit) + other * t, half], in_b.at[2 * q + t, half],
-            4 * q + 2 * t + half, send_b, recv_b, me + 2 * weight * (1 - 2 * bit),
+            q, send_b, recv_b, me + 2 * weight * (1 - 2 * bit),
         )
 
     def copy_c(i, half):
@@ -204,7 +204,7 @@
         _, _, bit, weight = orders_of[half]
         return halving(
             sum_b.at[2 * q + 1 - bit, half], in_c.at[q, half],
-            2 * q + half, send_c, recv_c, me + 2 * weight * (1 - 2 * bit),
+            q, send_c, recv_c, me + 2 * weight * (1 - 2 * bit),
         )
 
     def copy_d(q, half):
@@ -228,8 +228,8 @@
 
     def merge_a(i):
         q = turn(i)
+        stage_wait(in_a, 4 * q, 4, q, send_a, recv_a).wait_recv()
         for j in range(4):
-            copy_a(q, j).wait_recv()
             sum_a[4 * q + j] = added(gram[8 * q + 2 * j + bit0], in_a[4 * q + j])
         for half in range(2):
             for t in (1 - orders_of[half][2], orders_of[half][2]):
@@ -237,10 +237,10 @@
 
     def merge_b(i):
         q = turn(i)
+        stage_wait(in_b, 2 * q, 2, q, send_b, recv_b).wait_recv()
         for half in range(2):
             bit, weight, last, other = orders_of[half]
             for t in (1 - last, last):
-                copy_b(i, t, half).wait_recv()
                 sum_b[2 * q + t, half] = added(
                     sum_a[4 * q + weight * bit + other * t, half], in_b[2 * q + t, half]
                 )
@@ -248,17 +248,21 @@
 
     def merged_c(i, half):
         q = turn(i)
-        copy_c(i, half).wait_recv()
         return added(sum_b[2 * q + orders_of[half][2], half], in_c[q, half])
 
     def merge_c(i):
         q = turn(i)
+        stage_wait(in_c, q, 1, q, send_c, recv_c).wait_recv()
         for half in range(2):
             sum_c[q, half] = merged_c(i, half)
         copy_d(q, 0).start()
 
     def merge_x(i):
         copy_d(turn(i), 1).start()
+
+    def stage_wait(ref, first, count, index, sends, recvs):
+        view = ref.at[pl.ds(first, count)]
+        return halving(view, view, index, sends, recvs, partner)
 
     def start_a(i):
         for j in range(4):
@@ -393,9 +397,6 @@
     merge_c(cubes - 2)
     merge_x(cubes - 3)
     merge_x(cubes - 2)
-    for half in range(2):
-        gram_in[cube, half] = merged_c(cubes - 1, half)
-
     orders, places = [], []
     for b in range(blocks):
         order = (lax.broadcasted_iota(jnp.int32, (block, block), 0) == visit_ref[b:b + 1, :]).astype(F32)
@@ -431,6 +432,10 @@
     for b in range(blocks):
         inverse_c[b] = upright(inverse, b)
         margin_c[b] = upright(margin1, b)
+
+    stage_wait(in_c, cube, 1, cube, send_c, recv_c).wait_recv()
+    for half in range(2):
+        gram_in[cube, half] = merged_c(cubes - 1, half)
 
     wait_d(0).wait_recv()
     packed = jnp.sum(gram_in[:, 0].astype(F32), axis=0)
@@ -547,15 +552,9 @@
     wait_d(0).wait_send()
     wait_d(1).wait_send()
 
-    def drain(i):
-        for j in range(4):
-            copy_a(turn(i), j).wait_send()
-        for half in range(2):
-            for j in range(2):
-                copy_b(i, j, half).wait_send()
-            copy_c(i, half).wait_send()
-
-    loop(0, cubes, drain)
+    stage_wait(in_a, 0, 4 * cubes, 0, send_a, recv_a).wait_send()
+    stage_wait(in_b, 0, 2 * cubes, 0, send_b, recv_b).wait_send()
+    stage_wait(in_c, 0, cubes, 0, send_c, recv_c).wait_send()
 
 
 def split(packed, weights, alpha, objective):
@@ -590,7 +589,7 @@
         functools.partial(kernel, devices),
         name="svm_rounds",
         out_shape=jax.ShapeDtypeStruct((1, feats + rows + block), F32),
-        in_specs=[pl.BlockSpec(memory_space=pl.ANY)] * 8,
+        in_specs=[pl.BlockSpec(memory_space=pltpu.HBM)] * 8,
         out_specs=vmem,
         scratch_shapes=[
             pltpu.VMEM((owners, *span), F32), vectors(1, rows), vectors(1, rows), vectors(1, rows),
@@ -605,14 +604,17 @@
             grams(4 * cubes), grams(2 * cubes), grams(cubes), grams(cubes),
             pltpu.VMEM((GROUP // 2, block, 2 * block), BF16), pltpu.VMEM((2, blocks, GROUP, block, block), F32),
             pltpu.VMEM((block, block), F32), *[pltpu.VMEM((blocks, block, block), F32)] * 6,
-            semaphores(cubes), semaphores(7), semaphores(8), semaphores(5), semaphores(3 * cubes), semaphores(4 * cubes), semaphores(4 * cubes),
-            semaphores(4 * cubes), semaphores(4 * cubes), semaphores(2 * cubes), semaphores(2 * cubes),
+            semaphores(cubes), semaphores(7), semaphores(8), semaphores(5), semaphores(3 * cubes),
+            semaphores(1), semaphores(cubes), semaphores(1), semaphores(cubes), semaphores(1), semaphores(cubes),
             semaphores(2), semaphores(2),
         ],
         compiler_params=pltpu.CompilerParams(
-            collective_id=0, has_side_effects=True, vmem_limit_bytes=63 * 1024 * 1024
+            collective_id=0, has_side_effects=True, vmem_limit_bytes=48 * 1024 * 1024
         ),
-    )(data_t, labels, bound, *tiles, w_start[None], alpha_start[None], visit_order)
+    )(*[
+        pltpu.with_memory_space_constraint(x, pltpu.HBM)
+        for x in (data_t, labels, bound, *tiles, w_start[None], alpha_start[None], visit_order)
+    ])
     weights, alpha, objective = pl.pallas_call(
         split,
         name="split",
@@ -621,6 +623,7 @@
         ),
         in_specs=[vmem],
         out_specs=(vmem, vmem, vmem),
+        compiler_params=pltpu.CompilerParams(vmem_limit_bytes=1024 * 1024),
     )(out)
     return weights[0], alpha[0], objective[0, 0]
 

time: 43.5 us -> 41.5 us (0.954)
  Pallas kernels: 42.7 us -> 40.7 us
    pallas_call x1, Pallas kernels: 41.4 us -> 40.1 us  [body(): pl.pallas_call(functools.partial(kernel, devices), name='svm_rounds', out...]
    pallas_call x1, Pallas kernels: 1.24 us -> 0.57 us  [body(): pl.pallas_call(split, name='split', out_shape=(jax.ShapeDtypeStruct((1, f...]
where the time goes in v4:
time: 41.5 us; the launch traced here: 41.3 us
  Pallas kernels  40.7 us (98%)
  between operations  0.64 us (2%)
    pallas_call x1, Pallas kernels, body(): pl.pallas_call(functools.partial(kernel, devices), name='svm_rounds', out...  40.1 us

profile of v4, /device:TPU:0, one launch (start us, length us, event | category | flops | bytes accessed | tf_op | source)
XLA Modules:
  0.0 41.3 jit_solution(13105819091781714148)
XLA Ops:
  0.6 40.1 %svm_rounds.1.packed = f32[1,640]{1,0:T(1,128)S(1)} custom-call(bf16[256,8192]{1,0:T(8,128)(2,1)} %data_hbm.1, s32[32,1,256]{2,1,0:T(1,128)} %bitcast.9, f32[32,1,256]{2,1,0:T(1,128)} %bitcast.11, s32[8,8,128]{2,1,0:T(8,128)} %bitcast.10, f32[8,8,128]{2,1,0:T(8,128)} %bitcast.12, f32[1,256]{1,0:T(1,128)} %bitcast.13, f32[1,256]{1,0:T(1,128)} %bitcast.14, ...), custom_call_target="tpu_custom_call" | custom-call | tf_op jit(solution)/shard_map/svm_rounds/pallas_call | solution.py:588
  40.8 0.6 %split.1 = (f32[1,256]{1,0:T(1,128)}, f32[1,256]{1,0:T(1,128)}, f32[1,1]{1,0:T(1,128)}) custom-call(f32[1,640]{1,0:T(1,128)S(1)} %svm_rounds.1.packed), custom_call_target="tpu_custom_call" | custom-call | tf_op jit(solution)/shard_map/split/pallas_call | solution.py:618

commit v5 on v4

--- a/solution.py
+++ b/solution.py
@@ -98,7 +98,7 @@
 
     def gather_start(own, everyone, phase):
         everyone[me] = own[...]
-        spot = (phase - 3) * cubes + cube
+        spot = (phase - 3) * cubes - 2 * low + cube
         peers(lambda peer: remote(own, everyone.at[me], send_sem.at[phase], gather_sem.at[spot], peer).start())
 
     def part_of(lhs, part, q):
@@ -123,7 +123,7 @@
     def back(everyone, phase, meanwhile=None):
         def arrival(q, count):
             view = everyone.at[pl.ds(8 * q, count)]
-            spot = (phase - 3) * cubes + q
+            spot = (phase - 3) * cubes - 2 * low + q
             remote(view, view, send_sem.at[phase], gather_sem.at[spot], partner).wait_recv()
 
         def cube_sum(q, total):
@@ -209,14 +209,14 @@
 
     def copy_d(q, half):
         return pltpu.make_async_remote_copy(
-            src_ref=sum_c.at[q, half], dst_ref=gram_in.at[cube, half], send_sem=gram_send.at[half],
+            src_ref=sum_c.at[q, half], dst_ref=gram_in.at[cube, half], send_sem=gram_send.at[0],
             recv_sem=gram_recv.at[half], device_id=(me + 8 * (q - cube),), device_id_type=MESH,
         )
 
     def wait_d(half):
         view = gram_in.at[pl.ds(0, cubes - 1), half]
         return pltpu.make_async_remote_copy(
-            src_ref=view, dst_ref=view, send_sem=gram_send.at[half], recv_sem=gram_recv.at[half],
+            src_ref=view, dst_ref=view, send_sem=gram_send.at[0], recv_sem=gram_recv.at[half],
             device_id=(partner,), device_id_type=MESH,
         )
 
@@ -345,7 +345,7 @@
         side = owned_label[...].astype(F32)
         own0[...] = (owned_bound[...] * side * jnp.maximum(0.0, 1.0 - side * margin0)).astype(BF16)
         all0[mine] = own0[...]
-        peers(lambda peer: remote(own0, all0.at[mine], send_sem.at[3], gather_sem.at[cube], peer).start())
+        peers(lambda peer: remote(own0, all0.at[mine], send_sem.at[3], gather_sem.at[cube - low], peer).start())
 
     peers(scatter_send(part_d, got_d, 6))
     got_d[me] = part_d[me]
@@ -359,7 +359,7 @@
 
         def wait(count):
             view = all0.at[pl.ds(0, count)]
-            remote(view, view, send_sem.at[3], gather_sem.at[q], partner).wait_recv()
+            remote(view, view, send_sem.at[3], gather_sem.at[q - low], partner).wait_recv()
 
         own_turn = is_owner & (q == cube)
 
@@ -388,15 +388,10 @@
     merge_b(cubes - 2)
     merge_c(0)
 
-    def middle_step(i):
-        merge_c(i)
-        merge_x(i - 1)
-
-    loop(1, cubes - 2, middle_step)
+    loop(1, cubes - 2, merge_c)
     merge_b(cubes - 1)
     merge_c(cubes - 2)
-    merge_x(cubes - 3)
-    merge_x(cubes - 2)
+    loop(0, cubes - 1, merge_x)
     orders, places = [], []
     for b in range(blocks):
         order = (lax.broadcasted_iota(jnp.int32, (block, block), 0) == visit_ref[b:b + 1, :]).astype(F32)
@@ -549,8 +544,8 @@
     def _():
         waiting(part0, owners, send_sem.at[0], recv_sem.at[0]).wait_send()
 
-    wait_d(0).wait_send()
-    wait_d(1).wait_send()
+    view = gram_in.at[pl.ds(0, cubes - 1)]
+    remote(view, view, gram_send.at[0], gram_recv.at[0], partner).wait_send()
 
     stage_wait(in_a, 0, 4 * cubes, 0, send_a, recv_a).wait_send()
     stage_wait(in_b, 0, 2 * cubes, 0, send_b, recv_b).wait_send()
@@ -604,9 +599,9 @@
             grams(4 * cubes), grams(2 * cubes), grams(cubes), grams(cubes),
             pltpu.VMEM((GROUP // 2, block, 2 * block), BF16), pltpu.VMEM((2, blocks, GROUP, block, block), F32),
             pltpu.VMEM((block, block), F32), *[pltpu.VMEM((blocks, block, block), F32)] * 6,
-            semaphores(cubes), semaphores(7), semaphores(8), semaphores(5), semaphores(3 * cubes),
+            semaphores(cubes), semaphores(7), semaphores(8), semaphores(5), semaphores(3 * cubes - 2 * (cubes // 4)),
             semaphores(1), semaphores(cubes), semaphores(1), semaphores(cubes), semaphores(1), semaphores(cubes),
-            semaphores(2), semaphores(2),
+            semaphores(1), semaphores(2),
         ],
         compiler_params=pltpu.CompilerParams(
             collective_id=0, has_side_effects=True, vmem_limit_bytes=48 * 1024 * 1024

time: 41.5 us -> 41.4 us (level)
  no operation moved by 1% of the time
where the time goes in v5:
time: 41.4 us; the launch traced here: 41.3 us
  Pallas kernels  40.7 us (98%)
  between operations  0.64 us (2%)
    pallas_call x1, Pallas kernels, body(): pl.pallas_call(functools.partial(kernel, devices), name='svm_rounds', out...  40.1 us

profile of v5, /device:TPU:0, one launch (start us, length us, event | category | flops | bytes accessed | tf_op | source)
XLA Modules:
  0.0 41.3 jit_solution(16652454827620391098)
XLA Ops:
  0.6 40.1 %svm_rounds.1.packed = f32[1,640]{1,0:T(1,128)S(1)} custom-call(bf16[256,8192]{1,0:T(8,128)(2,1)} %data_hbm.1, s32[32,1,256]{2,1,0:T(1,128)} %bitcast.9, f32[32,1,256]{2,1,0:T(1,128)} %bitcast.11, s32[8,8,128]{2,1,0:T(8,128)} %bitcast.10, f32[8,8,128]{2,1,0:T(8,128)} %bitcast.12, f32[1,256]{1,0:T(1,128)} %bitcast.13, f32[1,256]{1,0:T(1,128)} %bitcast.14, ...), custom_call_target="tpu_custom_call" | custom-call | tf_op jit(solution)/shard_map/svm_rounds/pallas_call | solution.py:583
  40.7 0.6 %split.1 = (f32[1,256]{1,0:T(1,128)}, f32[1,256]{1,0:T(1,128)}, f32[1,1]{1,0:T(1,128)}) custom-call(f32[1,640]{1,0:T(1,128)S(1)} %svm_rounds.1.packed), custom_call_target="tpu_custom_call" | custom-call | tf_op jit(solution)/shard_map/split/pallas_call | solution.py:613
